TPU v7x, 128 devices: a whole 4x4x4 slice. The times are simulated.
128 devices in a mesh: row: 16 (over y_hi, z, core), col: 8 (over y_lo, x).
Axes of the slice: x: 4, y: 4 (y_hi: 2, y_lo: 2; y = y_hi * 2 + y_lo), z: 4, core: 2. Of those that a mesh axis runs over, the one named last changes fastest.
Arguments:
- vectors: float32 [49152, 128], P(('row', 'col')), may hold values from -6 to 6
- energies: float32 [49152], P(('row', 'col')), may hold values from 1 to 3
- intersections: bfloat16 [384, 512, 128], P(('row', 'col')), may hold values from -0.25 to 0.25
- coarse: bfloat16 [16, 16, 512, 512], P('col', 'row'), may hold values from -0.078125 to 0.078125
- fine_coarse: int32 [384], replicated, may hold values from 0 to 15, as said below
- coarse_slot: int32 [16], replicated, may hold values from 0 to 15, each once
- tile_codes: int32 [128, 432], P(('row', 'col')), may hold values from 0 to 1151, as said below
- tile_count: int32 [128], P(('row', 'col')), may hold values from 54 to 432, as said below
Outputs:
- first_step: float32 [49152, 128], P(('row', 'col'))
- second_step: float32 [49152, 128], P(('row', 'col'))
Inputs may be any that keep to these rules, and one draw needn't show every extreme that they name: `fine_coarse`: fine block k lies on device d = k // 3; with c = d % (8) its coarse k-point lies in c * 2 to (c + 1) * 2 - 1. `coarse_slot`: each coarse k-point has its own position. `tile_codes`: each row lists distinct codes; a code e stands for output position e // (C 3) and input position e % (C 3) of the device's lists, with C = 8. Only the first tile_count[d] codes of row d are used; some device uses all 432.
All inputs are finite; a program needn't handle non-finite values.
Results may differ from a plain program's by a relative error of at most 0.0044.
Values may be sent and summed in bfloat16 or wider, within the bound.
A program may use at most 128 MiB of HBM per device.

v0:
```python
import jax
import jax.numpy as jnp
from jax import lax
from jax.sharding import PartitionSpec as P

spectrum_center = 2.0
spectrum_half = 3.0
tile_batch = 16


def joined_along(parts, dim):
    dims = list(parts.shape[1:])
    dims[dim] *= parts.shape[0]
    return jnp.moveaxis(parts, 0, dim).reshape(dims)


def sent_to_all(value, axis):
    copies = jnp.broadcast_to(value, (lax.axis_size(axis), *value.shape))
    return lax.all_to_all(copies, axis, split_axis=0, concat_axis=0, tiled=True)


def gather_directly(value, axis, dim):
    return joined_along(sent_to_all(value, axis), dim)


def in_blocks_2(value, dim, length):
    before, after = (value.shape[:dim], value.shape[dim + 1 :])
    return jnp.moveaxis(value.reshape(*before, length, -1, *after), dim, 0)


def summed_on_arrival(value, axis, dim):
    parts = in_blocks_2(value, dim, lax.axis_size(axis))
    arrived = lax.all_to_all(parts, axis, split_axis=0, concat_axis=0, tiled=True)
    return arrived.sum(axis=0)


def lookup(values_table, positions):
    matches = positions[:, None] == jnp.arange(values_table.shape[0], dtype=jnp.int32)[None, :]
    return jnp.sum(jnp.where(matches, values_table[None, :], 0), axis=1)


def on_device(
    vectors, energies, intersections, coarse, fine_coarse, coarse_slot, tile_codes, tile_count
):
    rows_count = lax.axis_size("row")
    cols_count = lax.axis_size("col")
    row_id = lax.axis_index("row")
    col_id = lax.axis_index("col")
    blocks_dev = intersections.shape[0]
    pairs_coarse = intersections.shape[1]
    tile_side = intersections.shape[2]
    width_vec = vectors.shape[1]
    points_col = coarse.shape[0]
    spread = cols_count * blocks_dev
    depth_out = rows_count * blocks_dev
    index_out = jnp.arange(depth_out, dtype=jnp.int32)
    index_in = jnp.arange(spread, dtype=jnp.int32)
    out_blocks = (
        index_out // blocks_dev * cols_count + col_id
    ) * blocks_dev + index_out % blocks_dev
    in_blocks = (row_id * cols_count + index_in // blocks_dev) * blocks_dev + index_in % blocks_dev
    over_out = lax.all_gather(intersections, "row", axis=0, tiled=True)
    over_in = lax.all_gather(intersections, "col", axis=0, tiled=True)
    in_slots = lookup(coarse_slot, lookup(fine_coarse, in_blocks))
    coarse_strip = lax.all_gather(coarse, "row", axis=1, tiled=True)
    picked = jnp.take(coarse_strip, in_slots, axis=1)
    projected = jnp.einsum(
        "aicd,idt->iact", picked, over_in, preferred_element_type=jnp.float32
    ).astype(jnp.bfloat16)
    projected_flat = projected.reshape(spread * points_col, pairs_coarse, tile_side)
    out_points = lookup(fine_coarse, out_blocks) - col_id * points_col
    tile_total = tile_count[0]
    slot_ids = jnp.arange(tile_codes.shape[1], dtype=jnp.int32)
    sort_keys = jnp.where(slot_ids < tile_total, tile_codes[0], depth_out * spread + slot_ids)
    ordering = jnp.argsort(sort_keys, stable=True)
    tile_list = jnp.take(tile_codes[0], ordering, axis=0)
    sorted_out = jnp.where(slot_ids < tile_total, tile_list // spread, depth_out)
    groups = (tile_total + tile_batch - 1) // tile_batch

    def make_tiles(offset):
        part_codes = lax.dynamic_slice_in_dim(tile_list, offset, tile_batch)
        out_idx = part_codes // spread
        in_idx = part_codes % spread
        local_point = lookup(out_points, out_idx)
        left_over = jnp.take(over_out, out_idx, axis=0)
        right_sel = jnp.take(projected_flat, in_idx * points_col + local_point, axis=0)
        fresh_tiles = jnp.einsum(
            "kct,kcu->ktu", left_over, right_sel, preferred_element_type=jnp.float32
        ).astype(jnp.bfloat16)
        live_mask = offset + jnp.arange(tile_batch, dtype=jnp.int32) < tile_total
        return (
            jnp.where(live_mask[:, None, None], fresh_tiles, jnp.zeros_like(fresh_tiles)),
            out_idx,
            in_idx,
        )

    def fill_group(group, buffer):
        fresh_tiles = make_tiles(group * tile_batch)[0]
        return lax.dynamic_update_slice_in_dim(buffer, fresh_tiles, group * tile_batch, 0)

    stored = lax.fori_loop(
        0, groups, fill_group, jnp.zeros((tile_list.shape[0], tile_side, tile_side), jnp.bfloat16)
    )

    def partial_range(pieces, start, count):
        first_tile = jnp.sum((sorted_out < start).astype(jnp.int32))
        last_tile = jnp.sum((sorted_out < start + count).astype(jnp.int32))
        first_group = first_tile // tile_batch
        last_group = (last_tile + tile_batch - 1) // tile_batch

        def add_group(group, partial_value):
            offset = group * tile_batch
            fresh_tiles = lax.dynamic_slice_in_dim(stored, offset, tile_batch)
            part_codes = lax.dynamic_slice_in_dim(tile_list, offset, tile_batch)
            out_idx = part_codes // spread
            in_idx = part_codes % spread
            inputs = jnp.take(pieces, in_idx, axis=0)
            product = jnp.einsum(
                "ktu,kun->ktn", fresh_tiles, inputs, preferred_element_type=jnp.float32
            )
            local_out = out_idx - start
            inside = (local_out >= 0) & (local_out < count)
            product = jnp.where(inside[:, None, None], product, jnp.zeros_like(product))
            return partial_value.at[jnp.clip(local_out, 0, count - 1)].add(product)

        return lax.fori_loop(
            first_group,
            last_group,
            add_group,
            jnp.zeros((count, tile_side, width_vec), jnp.float32),
        )

    def apply_kernel(field):
        pieces = gather_directly(field.astype(jnp.bfloat16), "col", 0)
        partial_value = partial_range(pieces, 0, depth_out)
        return summed_on_arrival(partial_value, "row", 0)

    start_vec = vectors.reshape(blocks_dev, tile_side, width_vec)
    pair_energy = energies.reshape(blocks_dev, tile_side, 1)

    def apply_shifted(field):
        return (pair_energy * field + apply_kernel(field) - spectrum_center * field) / spectrum_half

    first_step = apply_shifted(start_vec)
    second_step = 2.0 * apply_shifted(first_step) - start_vec
    return (
        first_step.reshape(blocks_dev * tile_side, width_vec),
        second_step.reshape(blocks_dev * tile_side, width_vec),
    )


def solution(mesh):
    in_specs = (
        P(("row", "col"), None),
        P(("row", "col")),
        P(("row", "col"), None, None),
        P("col", "row", None, None),
        P(),
        P(),
        P(("row", "col"), None),
        P(("row", "col")),
    )
    out_specs = (P(("row", "col"), None), P(("row", "col"), None))
    return jax.shard_map(
        on_device, mesh=mesh, in_specs=in_specs, out_specs=out_specs, check_vma=False
    )
```

profile of v0, /device:TPU:111, one launch (start us, length us, event | category | flops | bytes accessed | tf_op | source)
XLA Modules:
  0.0 1029.5 jit_solution(15302442377119340710)
XLA Ops:
  11.4 5.1 all-to-all-start
  17.2 3.8 sort.17
  21.0 3.1 gather_fusion.4
  28.7 92.2 %all-gather.6.cloned.1.call-done = bf16[2,16,512,512]{3,2,1,0:T(8,128)(2,1)} async-done(((bf16[2,1,512,512]{3,2,1,0:T(8,128)(2,1)}), bf16[2,16,512,512]{3,2,1,0:T(8,128)(2,1)}) %all-gather.6.cloned.1.call-update) | async-done | bytes 16777232 | tf_op jit(solution)/shard_map/all_gather | solution.py:65
  120.9 16.0 %gather_fusion.5 = bf16[24,2,512,512]{3,2,1,0:T(8,128)(2,1)} fusion(bf16[2,16,512,512]{3,2,1,0:T(8,128)(2,1)} %all-gather.6.cloned.1.call-done, s32[1024]{0:T(1024)S(1)} %pad_clamp_fusion.4), kind=kCustom, calls=%fused_computation.5 | custom fusion | bytes 50331744 | tf_op jit(solution)/shard_map/jit(_take)/gather | solution.py:66
  136.9 26.1 %all-gather.8.cloned.1.call-done = bf16[24,512,128]{2,1,0:T(8,128)(2,1)} async-done(((bf16[3,512,128]{2,1,0:T(8,128)(2,1)}), bf16[24,512,128]{2,1,0:T(8,128)(2,1)}) %all-gather.8.cloned.1.call-update) | async-done | bytes 3145744 | tf_op jit(solution)/shard_map/all_gather | solution.py:63
  162.9 14.2 %fusion.41 = bf16[24,2,512,128]{3,2,1,0:T(8,128)(2,1)} fusion(bf16[24,2,512,512]{3,2,1,0:T(8,128)(2,1)} %gather_fusion.5, pred[24]{0:T(512)(128)(4,1)S(1)} %compare_and_fusion.6, bf16[24,512,128]{2,1,0:T(8,128)(2,1)} %all-gather.8.cloned.1.call-done), kind=kOutput, calls=%fused_computation.64 | convolution fusion | flops 3236954112 | bytes 34603032 | tf_op jit(solution)/shard_map/aicd,idt->iact/dot_general | solution.py:67
  177.1 53.1 %all-gather.4.cloned.1.call-done = bf16[48,512,128]{2,1,0:T(8,128)(2,1)} async-done(((bf16[3,512,128]{2,1,0:T(8,128)(2,1)}), bf16[48,512,128]{2,1,0:T(8,128)(2,1)}) %all-gather.4.cloned.1.call-update) | async-done | bytes 6291472 | tf_op jit(solution)/shard_map/all_gather | solution.py:62
  230.2 8.7 broadcast_in_dim.164
  238.9 117.5 %while.36 = (s32[]{:T(128)}, bf16[432,128,128]{2,1,0:T(8,128)(2,1)}, s32[]{:T(128)}, s32[]{:T(128)}, s32[432]{0:T(512)S(1)}, /*index=5*/bf16[48,512,128]{2,1,0:T...) while((s32[]{:T(128)}, ...), condition=%wide.region_8.10_spmd, body=%wide.region_6.9_spmd.sunk | while | flops 271061760 | bytes 13116695 | solution.py:101
  239.9 3.7 gather_fusion
  243.6 4.9 gather_fusion.1
  248.6 3.3 fusion.70
  252.9 3.7 gather_fusion
  256.7 4.9 gather_fusion.1
  261.6 3.3 fusion.70
  266.0 3.7 gather_fusion
  269.7 4.9 gather_fusion.1
  274.7 3.4 fusion.70
  279.0 3.7 gather_fusion
  282.8 4.9 gather_fusion.1
  287.7 3.3 fusion.70
  292.1 3.7 gather_fusion
  295.9 4.9 gather_fusion.1
  300.8 3.3 fusion.70
  305.1 3.7 gather_fusion
  308.9 4.9 gather_fusion.1
  313.8 3.3 fusion.70
  318.2 3.7 gather_fusion
  322.0 4.9 gather_fusion.1
  326.9 3.3 fusion.70
  331.2 3.7 gather_fusion
  335.0 4.9 gather_fusion.1
  339.9 3.3 fusion.70
  344.3 3.7 gather_fusion
  348.1 4.9 gather_fusion.1
  353.0 3.3 fusion.70
  356.3 2.0 broadcast.286.clone
  358.3 49.5 %while.37 = (s32[]{:T(128)}, f32[48,128,128]{2,1,0:T(8,128)}, s32[]{:T(128)}, s32[432]{0:T(512)S(1)}, bf16[432,128,128]{2,1,0:T(8,128)(2,1)}, /*index=5*/bf16[24...) while((s32[]{:T(128)}, f32[48,128,128]{2,1,0:T(8,128)}, s32[]{:T(128)}, ...), condition=%wide.region_11.14_spmd, body=%wide.region_9.13_spmd.sunk | while | flops 67896728 | bytes 6296283 | solution.py:126
  360.5 3.2 scatter_fusion
  366.0 3.3 scatter_fusion
  371.4 3.2 scatter_fusion
  376.9 3.3 scatter_fusion
  382.4 3.4 scatter_fusion
  388.0 3.2 scatter_fusion
  393.5 3.4 scatter_fusion
  399.0 3.2 scatter_fusion
  404.5 3.3 scatter_fusion
  407.8 386.0 %all_to_all.21 = f32[16,3,128,128]{3,2,1,0:T(8,128)S(1)} all-to-all(f32[16,3,128,128]{3,2,1,0:T(8,128)} %bitcast.44), channel_id=1, replica_groups=mesh['row'=16,'col'=8] {'row'}, dimensions={0} | all-to-all | bytes 6291456 | tf_op jit(solution)/shard_map/all_to_all | solution.py:33
  795.1 14.5 %all_to_all.20 = bf16[8,3,128,128]{3,2,1,0:T(8,128)(2,1)S(1)} all-to-all(bf16[8,3,128,128]{3,2,1,0:T(8,128)(2,1)S(1)} %broadcast_in_dim.174), channel_id=1, replica_groups=mesh['row'=16,'col'=8] {'col'}, dimensions={0} | all-to-all | bytes 1572864 | tf_op jit(solution)/shard_map/all_to_all | solution.py:19
  809.6 2.0 broadcast.286
  811.6 49.5 %while.38 = (s32[]{:T(128)}, f32[48,128,128]{2,1,0:T(8,128)}, s32[]{:T(128)}, s32[432]{0:T(512)S(1)}, bf16[432,128,128]{2,1,0:T(8,128)(2,1)}, /*index=5*/bf16[24...) while((s32[]{:T(128)}, f32[48,128,128]{2,1,0:T(8,128)}, s32[]{:T(128)}, ...), condition=%wide.region_15.18_spmd, body=%wide.region_13.17_spmd.sunk | while | flops 67896728 | bytes 6296283 | solution.py:126
  813.8 3.2 scatter_fusion.1
  819.3 3.3 scatter_fusion.1
  824.7 3.2 scatter_fusion.1
  830.2 3.3 scatter_fusion.1
  835.7 3.4 scatter_fusion.1
  841.3 3.2 scatter_fusion.1
  846.8 3.4 scatter_fusion.1
  852.3 3.2 scatter_fusion.1
  857.8 3.3 scatter_fusion.1
  861.1 112.9 %all-to-all-start.3 = ((f32[16,3,128,128]{3,2,1,0:T(8,128)}), f32[16,3,128,128]{3,2,1,0:T(8,128)S(1)}, u32[]{:S(2)}, u32[]{:S(2)}) async-start(f32[16,3,128,128]{3,2,1,0:T(8,128)} %bitcast.45), calls=%async_computation.3 | async-start | bytes 6291456 | tf_op jit(solution)/shard_map/all_to_all | solution.py:33
  974.1 46.3 %all-to-all-done.3 = f32[16,3,128,128]{3,2,1,0:T(8,128)S(1)} async-done(((f32[16,3,128,128]{3,2,1,0:T(8,128)}), f32[16,3,128,128]{3,2,1,0:T(8,128)S(1)}, u32[]{:S(2)}, u32[]{:S(2)}) %all-to-all-start.3) | async-done | bytes 3145760 | tf_op jit(solution)/shard_map/all_to_all | solution.py:33
  1021.2 1.8 fusion.47
  (183 shorter events, 55.6 us)
Async XLA Ops:
  7.2 10.0 copy-start
  7.2 113.7 %all-gather.6.cloned.1.call-start = ((), (), s32[]{:S(2)}) async-start(), calls=%async_computation.5 | async-start | bytes 17825792 | tf_op jit(solution)/shard_map/all_gather | solution.py:65
  7.9 20.3 %copy-start.3 = (s32[384]{0:T(512)S(1)}, s32[384]{0:T(512)}, u32[]{:S(2)}) copy-start(s32[384]{0:T(512)} %param.22) | copy-start | bytes 4612
  7.9 20.4 %copy-start.4 = (s32[16]{0:T(128)S(1)}, s32[16]{0:T(128)}, u32[]{:S(2)}) copy-start(s32[16]{0:T(128)} %param.23) | copy-start | bytes 196
  7.9 155.0 %all-gather.8.cloned.1.call-start = ((), (), s32[]{:S(2)}) async-start(), calls=%async_computation.6 | async-start | bytes 3538944 | tf_op jit(solution)/shard_map/all_gather | solution.py:63
  8.7 221.5 %all-gather.4.cloned.1.call-start = ((), (), s32[]{:S(2)}) async-start(), calls=%async_computation.4 | async-start | bytes 6684672 | tf_op jit(solution)/shard_map/all_gather | solution.py:62
  11.4 344.9 %all-to-all-start = ((bf16[8,3,128,128]{3,2,1,0:T(8,128)(2,1)}), bf16[8,3,128,128]{3,2,1,0:T(8,128)(2,1)S(1)}, u32[]{:S(2)}, u32[]{:S(2)}) async-start(bf16[8,3,128,128]{3,2,1,0:T(8,128)(2,1)} %broadcast_in_dim.173), calls=%async_computation | async-start | bytes 1572864 | tf_op jit(solution)/shard_map/all_to_all | solution.py:19
  793.9 0.9 copy-start.1
  793.9 0.9 copy-start.2
  861.1 159.2 %all-to-all-start.3 = ((f32[16,3,128,128]{3,2,1,0:T(8,128)}), f32[16,3,128,128]{3,2,1,0:T(8,128)S(1)}, u32[]{:S(2)}, u32[]{:S(2)}) async-start(f32[16,3,128,128]{3,2,1,0:T(8,128)} %bitcast.45), calls=%async_computation.3 | async-start | bytes 6291456 | tf_op jit(solution)/shard_map/all_to_all | solution.py:33
Sparse Core Ops, SparseCore 0:
  10.5 110.3 all-gather.5
  122.5 40.3 all-gather.7
  165.4 64.7 all-gather.3
where the time goes:
time: 1040 us; the launch traced here: 1030 us
  blocking collectives  401 us (39%)
  waiting for transfers between devices  220 us (21%)
  local copies, waits for them, and re-layouts  123 us (12%)
  starting transfers between devices  118 us (11%)
  other arithmetic  79.2 us (8%)
  matrix products  69.8 us (7%)
  between operations  17.8 us (2%)
    all_to_all x1, blocking collectives, summed_on_arrival(): lax.all_to_all(parts, axis, split_axis=0, concat_axis=0, tiled=True)  386 us
    all_to_all x1, starting transfers between devices, summed_on_arrival(): lax.all_to_all(parts, axis, split_axis=0, concat_axis=0, tiled=True)  113 us
    all_gather x1, waiting for transfers between devices, on_device(): coarse_strip = lax.all_gather(coarse, 'row', axis=1, tiled=True)  92.2 us
    scatter-add x18, other arithmetic, add_group(): return partial_value.at[jnp.clip(local_out, 0, count - 1)].add(product)  59.4 us
    all_gather x1, waiting for transfers between devices, on_device(): over_out = lax.all_gather(intersections, 'row', axis=0, tiled=True)  53.1 us
    all_to_all x1, waiting for transfers between devices, summed_on_arrival(): lax.all_to_all(parts, axis, split_axis=0, concat_axis=0, tiled=True)  46.3 us
    gather x9, local copies, waits for them, and re-layouts, make_tiles(): left_over = jnp.take(over_out, out_idx, axis=0)  44.3 us
    gather x9, local copies, waits for them, and re-layouts, make_tiles(): jnp.take(projected_flat, in_idx * points_col + local_point, axis=0)  33.6 us
  transfers between devices with their start and end apart: 5, of which 4 were waited for; matrix products, arithmetic and copies ran while one was open for 16% of the time, Pallas kernels for 0%

commit v1 on v0

v1 whole, which is shorter than its diff:
```python
import functools

import jax
import jax.numpy as jnp
from jax import lax
from jax.experimental import pallas as pl
from jax.experimental.pallas import tpu as pltpu
from jax.sharding import PartitionSpec as P

spectrum_center = 2.0
spectrum_half = 3.0
chunk_pairs = 16
unroll_pairs = 4


def lookup(values_table, positions):
    matches = positions[:, None] == jnp.arange(values_table.shape[0], dtype=jnp.int32)[None, :]
    return jnp.sum(jnp.where(matches, values_table[None, :], 0), axis=1)


def pair_tables(codes, count, depth_out, spread, points, pairs_max):
    slots = jnp.arange(codes.shape[0], dtype=jnp.int32)
    all_codes = jnp.arange(depth_out * spread, dtype=jnp.int32)
    hits = (codes[:, None] == all_codes[None, :]) & (slots < count)[:, None]
    mask = jnp.any(hits, axis=0).astype(jnp.int32).reshape(depth_out, spread)
    filled = jnp.sum(mask, axis=1)
    pairs = (filled + 1) // 2
    index_out = jnp.arange(depth_out, dtype=jnp.int32)
    index_in = jnp.arange(spread, dtype=jnp.int32)
    base = jnp.sum(jnp.where(index_out[None, :] < index_out[:, None], pairs[None, :], 0), axis=1)
    rank = jnp.sum(
        jnp.where(index_in[None, None, :] < index_in[None, :, None], mask[:, None, :], 0), axis=2
    )
    place = jnp.where(mask > 0, 2 * base[:, None] + rank, -1).reshape(-1)
    spots = jnp.arange(2 * pairs_max, dtype=jnp.int32)
    found = jnp.sum(
        jnp.where(spots[:, None] == place[None, :], all_codes[None, :] + 1, 0), axis=1
    )
    found = found.reshape(pairs_max, 2)
    live = found > 0
    code = jnp.maximum(found - 1, 0)
    out_idx = jnp.where(live[:, 0], code[:, 0] // spread, depth_out - 1)
    in_idx = jnp.where(live, code % spread, spread)
    point = lookup(points, out_idx)
    return out_idx, in_idx[:, 0], in_idx[:, 1], point, jnp.sum(pairs).reshape(1)


def add_pair(total_ref, fields_ref, tile, block, first, second):
    both = jnp.concatenate([fields_ref[first], fields_ref[second]], axis=0)
    return total_ref, block, jnp.dot(tile, both, preferred_element_type=jnp.float32)


def build_kernel(
    spread,
    slots_ref,
    out_ref_idx,
    first_idx,
    second_idx,
    point_idx,
    used_ref,
    coarse_ref,
    over_in_ref,
    over_out_ref,
    fields_ref,
    tiles_ref,
    partial_ref,
    projected_ref,
    total_ref,
):
    step = pl.program_id(0)
    points = coarse_ref.shape[0]

    @pl.when(step == 0)
    def _():
        total_ref[...] = jnp.zeros_like(total_ref)

    @pl.when(step < spread)
    def _():
        for a in range(points):
            projected_ref[step * points + a] = jnp.dot(
                coarse_ref[a, 0], over_in_ref[0], preferred_element_type=jnp.float32
            ).astype(jnp.bfloat16)

    start = (step - spread) * chunk_pairs

    @pl.when((step >= spread) & (start < used_ref[0]))
    def _():
        def group(g, carry):
            adds = []
            for k in range(unroll_pairs):
                local = g * unroll_pairs + k
                pair = start + local
                block, first, second = out_ref_idx[pair], first_idx[pair], second_idx[pair]
                a = point_idx[pair]
                left = jnp.minimum(first, spread - 1) * points + a
                right = jnp.minimum(second, spread - 1) * points + a
                both = jnp.concatenate([projected_ref[left], projected_ref[right]], axis=1)
                tile = jnp.dot(
                    over_out_ref[block], both, preferred_element_type=jnp.float32
                ).astype(jnp.bfloat16)
                tiles_ref[local] = tile
                adds.append(add_pair(total_ref, fields_ref, tile, block, first, second))
            for ref, block, product in adds:
                ref[block] += product
            return carry

        lax.fori_loop(0, chunk_pairs // unroll_pairs, group, 0)

    @pl.when(step == pl.num_programs(0) - 1)
    def _():
        partial_ref[...] = total_ref[...].astype(partial_ref.dtype)


def apply_kernel_body(
    out_ref_idx, first_idx, second_idx, used_ref, tiles_ref, fields_ref, partial_ref, total_ref
):
    step = pl.program_id(0)

    @pl.when(step == 0)
    def _():
        total_ref[...] = jnp.zeros_like(total_ref)

    start = step * chunk_pairs

    @pl.when(start < used_ref[0])
    def _():
        def group(g, carry):
            adds = []
            for k in range(unroll_pairs):
                local = g * unroll_pairs + k
                pair = start + local
                adds.append(
                    add_pair(
                        total_ref,
                        fields_ref,
                        tiles_ref[local],
                        out_ref_idx[pair],
                        first_idx[pair],
                        second_idx[pair],
                    )
                )
            for ref, block, product in adds:
                ref[block] += product
            return carry

        lax.fori_loop(0, chunk_pairs // unroll_pairs, group, 0)

    @pl.when(step == pl.num_programs(0) - 1)
    def _():
        partial_ref[...] = total_ref[...].astype(partial_ref.dtype)


def build_tiles(in_slots, tables, coarse_strip, over_in, over_out, fields, pairs_max):
    points, _, pairs_coarse, _ = coarse_strip.shape
    spread = over_in.shape[0]
    depth_out, tile_side, _ = over_out.shape
    width = fields.shape[2]
    chunks = pairs_max // chunk_pairs

    def tile_chunk(s, *refs):
        last = jnp.maximum((refs[5][0] + chunk_pairs - 1) // chunk_pairs - 1, 0)
        return (jnp.clip(s - spread, 0, last), 0, 0)

    def held(s, *refs):
        return (0, 0, 0)

    grid_spec = pltpu.PrefetchScalarGridSpec(
        num_scalar_prefetch=6,
        grid=(spread + chunks,),
        in_specs=[
            pl.BlockSpec(
                (points, 1, pairs_coarse, pairs_coarse),
                lambda s, slots, *refs: (0, slots[jnp.minimum(s, spread - 1)], 0, 0),
            ),
            pl.BlockSpec(
                (1, pairs_coarse, tile_side), lambda s, *refs: (jnp.minimum(s, spread - 1), 0, 0)
            ),
            pl.BlockSpec(over_out.shape, held),
            pl.BlockSpec(fields.shape, held),
        ],
        out_specs=[
            pl.BlockSpec((chunk_pairs, tile_side, 2 * tile_side), tile_chunk),
            pl.BlockSpec((depth_out, tile_side, width), held),
        ],
        scratch_shapes=[
            pltpu.VMEM((spread * points, pairs_coarse, tile_side), jnp.bfloat16),
            pltpu.VMEM((depth_out, tile_side, width), jnp.float32),
        ],
    )
    return pl.pallas_call(
        functools.partial(build_kernel, spread),
        grid_spec=grid_spec,
        out_shape=[
            jax.ShapeDtypeStruct((pairs_max, tile_side, 2 * tile_side), jnp.bfloat16),
            jax.ShapeDtypeStruct((depth_out, tile_side, width), jnp.bfloat16),
        ],
        compiler_params=pltpu.CompilerParams(vmem_limit_bytes=52 * 1024 * 1024),
        name="build_tiles",
    )(in_slots, *tables, coarse_strip, over_in, over_out, fields)


def apply_tiles(tables, tiles, fields, depth_out):
    pairs_max, tile_side, _ = tiles.shape
    width = fields.shape[2]
    out_idx, first, second, _, used = tables

    def tile_chunk(s, *refs):
        last = jnp.maximum((refs[3][0] + chunk_pairs - 1) // chunk_pairs - 1, 0)
        return (jnp.minimum(s, last), 0, 0)

    def held(s, *refs):
        return (0, 0, 0)

    grid_spec = pltpu.PrefetchScalarGridSpec(
        num_scalar_prefetch=4,
        grid=(pairs_max // chunk_pairs,),
        in_specs=[
            pl.BlockSpec((chunk_pairs, tile_side, 2 * tile_side), tile_chunk),
            pl.BlockSpec(fields.shape, held),
        ],
        out_specs=pl.BlockSpec((depth_out, tile_side, width), held),
        scratch_shapes=[pltpu.VMEM((depth_out, tile_side, width), jnp.float32)],
    )
    return pl.pallas_call(
        apply_kernel_body,
        grid_spec=grid_spec,
        out_shape=jax.ShapeDtypeStruct((depth_out, tile_side, width), jnp.bfloat16),
        compiler_params=pltpu.CompilerParams(vmem_limit_bytes=32 * 1024 * 1024),
        name="apply_tiles",
    )(out_idx, first, second, used, tiles, fields)


def on_device(
    vectors, energies, intersections, coarse, fine_coarse, coarse_slot, tile_codes, tile_count
):
    rows_count = lax.axis_size("row")
    cols_count = lax.axis_size("col")
    row_id = lax.axis_index("row")
    col_id = lax.axis_index("col")
    blocks_dev, pairs_coarse, tile_side = intersections.shape
    width_vec = vectors.shape[1]
    points_col = coarse.shape[0]
    spread = cols_count * blocks_dev
    depth_out = rows_count * blocks_dev
    pairs_max = (tile_codes.shape[1] + depth_out) // 2
    pairs_max = -(-pairs_max // chunk_pairs) * chunk_pairs
    index_out = jnp.arange(depth_out, dtype=jnp.int32)
    index_in = jnp.arange(spread, dtype=jnp.int32)
    out_blocks = (
        index_out // blocks_dev * cols_count + col_id
    ) * blocks_dev + index_out % blocks_dev
    in_blocks = (row_id * cols_count + index_in // blocks_dev) * blocks_dev + index_in % blocks_dev
    in_slots = lookup(coarse_slot, lookup(fine_coarse, in_blocks))
    out_points = lookup(fine_coarse, out_blocks) - col_id * points_col
    tables = pair_tables(
        tile_codes[0], tile_count[0], depth_out, spread, out_points, pairs_max
    )

    coarse_strip = lax.all_gather(coarse, "row", axis=1, tiled=True)
    over_in = lax.all_gather(intersections, "col", axis=0, tiled=True)
    over_out = lax.all_gather(jnp.swapaxes(intersections, 1, 2), "row", axis=0, tiled=True)

    def gathered(field):
        rounded = field.astype(jnp.bfloat16)
        copies = jnp.broadcast_to(rounded, (cols_count, *rounded.shape))
        pieces = lax.all_to_all(copies, "col", split_axis=0, concat_axis=0, tiled=True)
        pieces = pieces.reshape(spread, tile_side, width_vec)
        return jnp.pad(pieces, ((0, 1), (0, 0), (0, 0)))

    def summed(partial):
        parts = partial.reshape(rows_count, blocks_dev, tile_side, width_vec)
        arrived = lax.all_to_all(parts, "row", split_axis=0, concat_axis=0, tiled=True)
        return jnp.sum(arrived.astype(jnp.float32), axis=0)

    start_vec = vectors.reshape(blocks_dev, tile_side, width_vec)
    pair_energy = energies.reshape(blocks_dev, tile_side, 1)

    def shifted(field, kernel_part):
        return (pair_energy * field + kernel_part - spectrum_center * field) / spectrum_half

    tiles, partial = build_tiles(
        in_slots, tables, coarse_strip, over_in, over_out, gathered(start_vec), pairs_max
    )
    first_step = shifted(start_vec, summed(partial))
    partial = apply_tiles(tables, tiles, gathered(first_step), depth_out)
    second_step = 2.0 * shifted(first_step, summed(partial)) - start_vec
    return (
        first_step.reshape(blocks_dev * tile_side, width_vec),
        second_step.reshape(blocks_dev * tile_side, width_vec),
    )


def solution(mesh):
    in_specs = (
        P(("row", "col"), None),
        P(("row", "col")),
        P(("row", "col"), None, None),
        P("col", "row", None, None),
        P(),
        P(),
        P(("row", "col"), None),
        P(("row", "col")),
    )
    out_specs = (P(("row", "col"), None), P(("row", "col"), None))
    return jax.shard_map(
        on_device, mesh=mesh, in_specs=in_specs, out_specs=out_specs, check_vma=False
    )
```

time: 1040 us -> 409 us (0.39)
  the two profiles are of different devices: /device:TPU:111 before, /device:TPU:1 now
where the time goes in v1:
time: 409 us; the launch traced here: 408 us
  waiting for transfers between devices  240 us (59%)
  blocking collectives  73.2 us (18%)
  Pallas kernels  50.7 us (12%)
  starting transfers between devices  15 us (4%)
  between operations  14.7 us (4%)
  local copies, waits for them, and re-layouts  9.73 us (2%)
  other arithmetic  4.27 us (1%)
    all_gather x1, waiting for transfers between devices, on_device(): coarse_strip = lax.all_gather(coarse, 'row', axis=1, tiled=True)  109 us
    all_gather x1, waiting for transfers between devices, on_device(): lax.all_gather(jnp.swapaxes(intersections, 1, 2), 'row', axis=0, tiled=True)  68.8 us
    pallas_call x1, Pallas kernels, build_tiles(): pl.pallas_call(functools.partial(build_kernel, spread), grid_spec=grid_sp...  42.8 us
    all_to_all x1, blocking collectives, summed(): lax.all_to_all(parts, 'row', split_axis=0, concat_axis=0, tiled=True)  37.7 us
    all_to_all x1, blocking collectives, gathered(): lax.all_to_all(copies, 'col', split_axis=0, concat_axis=0, tiled=True)  35.5 us
    all_gather x1, waiting for transfers between devices, on_device(): over_in = lax.all_gather(intersections, 'col', axis=0, tiled=True)  26 us
    all_to_all x1, waiting for transfers between devices, summed(): lax.all_to_all(parts, 'row', split_axis=0, concat_axis=0, tiled=True)  22.7 us
    all_to_all x1, waiting for transfers between devices, gathered(): lax.all_to_all(copies, 'col', split_axis=0, concat_axis=0, tiled=True)  12.1 us
  transfers between devices with their start and end apart: 5, of which 5 were waited for; matrix products, arithmetic and copies ran while one was open for 2% of the time, Pallas kernels for 0%

profile of v1, /device:TPU:1, one launch (start us, length us, event | category | flops | bytes accessed | tf_op | source)
XLA Modules:
  0.0 407.7 jit_solution(5908480165177975931)
XLA Ops:
  7.2 0.0 copy-start.1
  7.2 0.0 all-gather.6.cloned.1.call-start
  7.2 0.7 all-gather.6.cloned.1.call-update
  7.9 0.0 all-gather.8.cloned.1.call-start
  8.0 1.9 copy.15
  9.9 0.0 copy-start.4
  9.9 0.0 all-gather.8.cloned.1.call-update
  9.9 0.0 copy-start.3
  9.9 0.0 copy-start.5
  9.9 0.0 all-gather.4.cloned.1.call-start
  10.0 0.7 all-gather.4.cloned.1.call-update
  10.7 0.0 copy-done.1
  10.7 1.1 broadcast_in_dim.150
  11.7 5.9 %all-to-all-start = ((bf16[8,3,128,128]{3,2,1,0:T(8,128)(2,1)}), bf16[8,3,128,128]{3,2,1,0:T(8,128)(2,1)S(1)}, u32[]{:S(2)}, u32[]{:S(2)}) async-start(bf16[8,3,128,128]{3,2,1,0:T(8,128)(2,1)} %broadcast_in_dim.150), calls=%async_computation | async-start | bytes 1572864 | tf_op jit(solution)/shard_map/all_to_all | solution.py:266
  18.3 0.0 copy-done.4
  18.3 0.3 fusion.1
  18.6 0.1 reshape.177
  18.7 0.1 copy.13
  18.8 0.1 reduce_sum.105
  18.9 0.6 fusion.20
  19.5 0.1 select_reduce_fusion.5
  19.7 0.2 select_reduce_fusion.1
  19.9 0.1 copy.14
  19.9 0.1 add.138
  20.0 0.3 select_reduce_fusion
  20.3 0.2 gt.19
  20.5 0.1 max.7
  20.7 0.2 fusion.9
  20.9 0.1 reduce.1
  21.1 0.0 copy-done.3
  21.1 0.2 select_reduce_fusion.4
  21.3 0.0 copy-done.5
  21.3 0.1 select_reduce_fusion.6.slots_ref
  21.4 0.2 select_reduce_fusion.2
  21.5 0.1 select_reduce_fusion.3.point_idx
  21.6 0.1 slice_reduce_fusion.2
  21.8 0.1 fusion.7
  21.8 0.2 slice_reduce_fusion
  22.1 12.1 %all-to-all-done = bf16[8,3,128,128]{3,2,1,0:T(8,128)(2,1)S(1)} async-done(((bf16[8,3,128,128]{3,2,1,0:T(8,128)(2,1)}), bf16[8,3,128,128]{3,2,1,0:T(8,128)(2,1)S(1)}, u32[]{:S(2)}, u32[]{:S(2)}) %all-to-all-start) | async-done | bytes 786464 | tf_op jit(solution)/shard_map/all_to_all | solution.py:266
  34.2 0.1 pad.7.fields_ref
  34.2 26.0 %all-gather.6.cloned.1.call-done.over_in_ref = bf16[24,512,128]{2,1,0:T(8,128)(2,1)} async-done(((bf16[3,512,128]{2,1,0:T(8,128)(2,1)}), bf16[24,512,128]{2,1,0:T(8,128)(2,1)}) %all-gather.6.cloned.1.call-update) | async-done | bytes 3145744 | tf_op jit(solution)/shard_map/all_gather | solution.py:260
  60.3 68.8 %all-gather.8.cloned.1.call-done.over_out_ref = bf16[48,128,512]{2,1,0:T(8,128)(2,1)} async-done(((bf16[3,128,512]{2,1,0:T(8,128)(2,1)}), bf16[48,128,512]{2,1,0:T(8,128)(2,1)}) %all-gather.8.cloned.1.call-update) | async-done | bytes 6291472 | tf_op jit(solution)/shard_map/all_gather | solution.py:261
  129.1 109.1 %all-gather.4.cloned.1.call-done.coarse_ref = bf16[2,16,512,512]{3,2,1,0:T(8,128)(2,1)} async-done(((bf16[2,1,512,512]{3,2,1,0:T(8,128)(2,1)}), bf16[2,16,512,512]{3,2,1,0:T(8,128)(2,1)}) %all-gather.4.cloned.1.call-update) | async-done | bytes 16777232 | tf_op jit(solution)/shard_map/all_gather | solution.py:259
  238.2 42.8 %build_tiles.1 = (bf16[240,128,256]{2,1,0:T(8,128)(2,1)}, bf16[48,128,128]{2,1,0:T(8,128)(2,1)}) custom-call(s32[24]{0:T(128)S(1)} %select_reduce_fusion.6.slots_ref, s32[240]{0:T(256)S(1)} %fusion.12.out_ref_idx, s32[240]{0:T(256)S(1)} %get-tuple-element.9.first_idx, s32[240]{0:T(256)S(1)} %get-tuple-element.8.second_idx, ...), custom_call_target="tpu_custom_call" | custom-call | tf_op jit(solution)/shard_map/build_tiles/pallas_call | solution.py:190
  281.0 0.0 copy-start.2
  281.0 37.7 %all_to_all.20 = bf16[16,3,128,128]{3,2,1,0:T(8,128)(2,1)S(1)} all-to-all(bf16[16,3,128,128]{3,2,1,0:T(8,128)(2,1)} %bitcast.31), channel_id=1, replica_groups=mesh['row'=16,'col'=8] {'row'}, dimensions={0} | all-to-all | bytes 3145728 | tf_op jit(solution)/shard_map/all_to_all | solution.py:272
  318.7 0.3 convert_reduce_fusion.1
  319.0 0.0 copy-done.2
  319.0 0.1 multiply_convert_fusion
  319.1 0.2 broadcast_in_dim.151
  319.3 35.5 %all_to_all.21 = bf16[8,3,128,128]{3,2,1,0:T(8,128)(2,1)S(1)} all-to-all(bf16[8,3,128,128]{3,2,1,0:T(8,128)(2,1)S(1)} %broadcast_in_dim.151), channel_id=1, replica_groups=mesh['row'=16,'col'=8] {'col'}, dimensions={0} | all-to-all | bytes 1572864 | tf_op jit(solution)/shard_map/all_to_all | solution.py:266
  354.8 0.1 pad.8.fields_ref
  354.9 0.0 copy-start
  354.9 5.5 %copy-done = bf16[240,128,256]{2,1,0:T(8,128)(2,1)S(1)} copy-done((bf16[240,128,256]{2,1,0:T(8,128)(2,1)S(1)}, bf16[240,128,256]{2,1,0:T(8,128)(2,1)}, u32[]{:S(2)}) %copy-start) | copy-done | bytes 15728664
  360.4 7.9 %apply_tiles.1 = bf16[48,128,128]{2,1,0:T(8,128)(2,1)} custom-call(s32[240]{0:T(256)S(1)} %fusion.12.out_ref_idx, s32[240]{0:T(256)S(1)} %get-tuple-element.9.first_idx, s32[240]{0:T(256)S(1)} %get-tuple-element.8.second_idx, s32[1]{0:T(128)} %bitcast.2.used_ref, bf16[240,128,256]{2,1,0:T(8,128)(2,1)S(1)} %copy-done, bf16[25,128,128]{2,1,0:T(8,128)(2,1)S(1)} %pad.8.fields_ref), custom_call_target="tpu_custom_call" | custom-call | tf_op jit(solution)/shard_map/apply_tiles/pallas_call | solution.py:224
  368.2 9.1 %all-to-all-start.3 = ((bf16[16,3,128,128]{3,2,1,0:T(8,128)(2,1)}), bf16[16,3,128,128]{3,2,1,0:T(8,128)(2,1)S(1)}, u32[]{:S(2)}, u32[]{:S(2)}) async-start(bf16[16,3,128,128]{3,2,1,0:T(8,128)(2,1)} %bitcast.10), calls=%async_computation.3 | async-start | bytes 3145728 | tf_op jit(solution)/shard_map/all_to_all | solution.py:272
  377.3 22.7 %all-to-all-done.3 = bf16[16,3,128,128]{3,2,1,0:T(8,128)(2,1)S(1)} async-done(((bf16[16,3,128,128]{3,2,1,0:T(8,128)(2,1)}), bf16[16,3,128,128]{3,2,1,0:T(8,128)(2,1)S(1)}, u32[]{:S(2)}, u32[]{:S(2)}) %all-to-all-start.3) | async-done | bytes 1572896 | tf_op jit(solution)/shard_map/all_to_all | solution.py:272
  400.0 0.3 convert_reduce_fusion
  400.3 0.9 fusion.4
  (14 shorter events, 0.1 us)
Async XLA Ops:
  7.2 3.5 copy-start.1
  7.2 53.1 %all-gather.6.cloned.1.call-start = ((), (), s32[]{:S(2)}) async-start(), calls=%async_computation.5 | async-start | bytes 3538944 | tf_op jit(solution)/shard_map/all_gather | solution.py:260
  7.9 121.2 %all-gather.8.cloned.1.call-start = ((), (), s32[]{:S(2)}) async-start(), calls=%async_computation.6 | async-start | bytes 6684672 | tf_op jit(solution)/shard_map/all_gather | solution.py:261
  9.9 8.4 %copy-start.4 = (s32[1,432]{1,0:T(1,128)S(1)}, s32[1,432]{1,0:T(1,128)}, u32[]{:S(2)}) copy-start(s32[1,432]{1,0:T(1,128)} %param.14) | copy-start | bytes 5188
  9.9 11.2 %copy-start.3 = (s32[384]{0:T(512)S(1)}, s32[384]{0:T(512)}, u32[]{:S(2)}) copy-start(s32[384]{0:T(512)} %param.12) | copy-start | bytes 4612
  9.9 11.4 %copy-start.5 = (s32[16]{0:T(128)S(1)}, s32[16]{0:T(128)}, u32[]{:S(2)}) copy-start(s32[16]{0:T(128)} %param.13) | copy-start | bytes 196
  9.9 228.3 %all-gather.4.cloned.1.call-start = ((), (), s32[]{:S(2)}) async-start(), calls=%async_computation.4 | async-start | bytes 17825792 | tf_op jit(solution)/shard_map/all_gather | solution.py:259
  11.7 22.4 %all-to-all-start = ((bf16[8,3,128,128]{3,2,1,0:T(8,128)(2,1)}), bf16[8,3,128,128]{3,2,1,0:T(8,128)(2,1)S(1)}, u32[]{:S(2)}, u32[]{:S(2)}) async-start(bf16[8,3,128,128]{3,2,1,0:T(8,128)(2,1)} %broadcast_in_dim.150), calls=%async_computation | async-start | bytes 1572864 | tf_op jit(solution)/shard_map/all_to_all | solution.py:266
  281.0 37.9 %copy-start.2 = (f32[384]{0:T(512)S(1)}, f32[384]{0:T(512)}, u32[]{:S(2)}) copy-start(f32[384]{0:T(512)} %param.9) | copy-start | bytes 4612
  354.9 5.5 %copy-start = (bf16[240,128,256]{2,1,0:T(8,128)(2,1)S(1)}, bf16[240,128,256]{2,1,0:T(8,128)(2,1)}, u32[]{:S(2)}) copy-start(bf16[240,128,256]{2,1,0:T(8,128)(2,1)} %get-tuple-element.5.tiles_ref) | copy-start | bytes 47185924
  368.2 31.8 %all-to-all-start.3 = ((bf16[16,3,128,128]{3,2,1,0:T(8,128)(2,1)}), bf16[16,3,128,128]{3,2,1,0:T(8,128)(2,1)S(1)}, u32[]{:S(2)}, u32[]{:S(2)}) async-start(bf16[16,3,128,128]{3,2,1,0:T(8,128)(2,1)} %bitcast.10), calls=%async_computation.3 | async-start | bytes 3145728 | tf_op jit(solution)/shard_map/all_to_all | solution.py:272
Sparse Core Ops, SparseCore 0:
  9.6 50.6 all-gather.5
  62.8 66.2 all-gather.7
  131.6 106.5 all-gather.3

commit v2 on v1

--- a/solution.py
+++ b/solution.py
@@ -11,6 +11,8 @@
 spectrum_half = 3.0
 chunk_pairs = 16
 unroll_pairs = 4
+gather_copies = 53
+MESH = pl.DeviceIdType.MESH
 
 
 def lookup(values_table, positions):
@@ -45,12 +47,22 @@
     return out_idx, in_idx[:, 0], in_idx[:, 1], point, jnp.sum(pairs).reshape(1)
 
 
+def block_of(ref, block, blocks_dev, side):
+    rows = pl.ds(pl.multiple_of(block % blocks_dev * side, side), side)
+    return ref[block // blocks_dev, rows, :]
+
+
 def add_pair(total_ref, fields_ref, tile, block, first, second):
-    both = jnp.concatenate([fields_ref[first], fields_ref[second]], axis=0)
+    blocks_dev = fields_ref.shape[1] // total_ref.shape[1]
+    side = total_ref.shape[1]
+    both = jnp.concatenate(
+        [block_of(fields_ref, place, blocks_dev, side) for place in (first, second)], axis=0
+    )
     return total_ref, block, jnp.dot(tile, both, preferred_element_type=jnp.float32)
 
 
 def build_kernel(
+    blocks_dev,
     spread,
     slots_ref,
     out_ref_idx,
@@ -58,28 +70,52 @@
     second_idx,
     point_idx,
     used_ref,
-    coarse_ref,
+    coarse_a_ref,
+    coarse_b_ref,
     over_in_ref,
-    over_out_ref,
-    fields_ref,
+    packed_a_ref,
+    packed_i_ref,
     tiles_ref,
     partial_ref,
     projected_ref,
     total_ref,
+    over_out_ref,
+    fields_ref,
+    sems,
 ):
     step = pl.program_id(0)
-    points = coarse_ref.shape[0]
+    side = total_ref.shape[1]
+    depth = coarse_a_ref.shape[1]
+    cols = packed_i_ref.shape[0]
+    copies = (
+        pltpu.make_async_copy(
+            packed_a_ref.at[:, pl.ds(depth, blocks_dev * side), :], over_out_ref, sems.at[0]
+        ),
+        pltpu.make_async_copy(
+            packed_i_ref.at[:, pl.ds(blocks_dev * depth, blocks_dev * side), :],
+            fields_ref.at[pl.ds(0, cols)],
+            sems.at[1],
+        ),
+    )
 
     @pl.when(step == 0)
     def _():
+        for copy in copies:
+            copy.start()
         total_ref[...] = jnp.zeros_like(total_ref)
+        fields_ref[cols] = jnp.zeros(fields_ref.shape[1:], fields_ref.dtype)
 
     @pl.when(step < spread)
     def _():
-        for a in range(points):
-            projected_ref[step * points + a] = jnp.dot(
-                coarse_ref[a, 0], over_in_ref[0], preferred_element_type=jnp.float32
+        for a, ref in enumerate((coarse_a_ref, coarse_b_ref)):
+            projected_ref[step * 2 + a] = jnp.dot(
+                ref[0], over_in_ref[0], preferred_element_type=jnp.float32
             ).astype(jnp.bfloat16)
+
+    @pl.when(step == spread)
+    def _():
+        for copy in copies:
+            copy.wait()
 
     start = (step - spread) * chunk_pairs
 
@@ -92,11 +128,13 @@
                 pair = start + local
                 block, first, second = out_ref_idx[pair], first_idx[pair], second_idx[pair]
                 a = point_idx[pair]
-                left = jnp.minimum(first, spread - 1) * points + a
-                right = jnp.minimum(second, spread - 1) * points + a
+                left = jnp.minimum(first, spread - 1) * 2 + a
+                right = jnp.minimum(second, spread - 1) * 2 + a
                 both = jnp.concatenate([projected_ref[left], projected_ref[right]], axis=1)
                 tile = jnp.dot(
-                    over_out_ref[block], both, preferred_element_type=jnp.float32
+                    block_of(over_out_ref, block, blocks_dev, side),
+                    both,
+                    preferred_element_type=jnp.float32,
                 ).astype(jnp.bfloat16)
                 tiles_ref[local] = tile
                 adds.append(add_pair(total_ref, fields_ref, tile, block, first, second))
@@ -112,13 +150,24 @@
 
 
 def apply_kernel_body(
-    out_ref_idx, first_idx, second_idx, used_ref, tiles_ref, fields_ref, partial_ref, total_ref
+    out_ref_idx,
+    first_idx,
+    second_idx,
+    used_ref,
+    tiles_ref,
+    pieces_ref,
+    partial_ref,
+    total_ref,
+    fields_ref,
 ):
     step = pl.program_id(0)
+    cols = pieces_ref.shape[0]
 
     @pl.when(step == 0)
     def _():
         total_ref[...] = jnp.zeros_like(total_ref)
+        fields_ref[pl.ds(0, cols)] = pieces_ref[...]
+        fields_ref[cols] = jnp.zeros(fields_ref.shape[1:], fields_ref.dtype)
 
     start = step * chunk_pairs
 
@@ -150,58 +199,207 @@
         partial_ref[...] = total_ref[...].astype(partial_ref.dtype)
 
 
-def build_tiles(in_slots, tables, coarse_strip, over_in, over_out, fields, pairs_max):
-    points, _, pairs_coarse, _ = coarse_strip.shape
-    spread = over_in.shape[0]
-    depth_out, tile_side, _ = over_out.shape
-    width = fields.shape[2]
+def gather_kernel(a_ref, b_ref, i_ref, out_a, out_b, out_i, send_sem, recv_sem, own_sem):
+    row, col = lax.axis_index("row"), lax.axis_index("col")
+    h, z, k = row // 8, row // 2 % 4, row % 2
+    l, x = col // 4, col % 4
+
+    def row_of(hh, zz):
+        return (hh * 4 + zz % 4) * 2 + k
+
+    partner = (row_of(1 - h, z), col)
+    z_dev = ((row_of(h, z + 1), col), (row_of(h, z + 3), col))
+    x_dev = ((row, l * 4 + (x + 1) % 4), (row, l * 4 + (x + 3) % 4))
+    sibling = (row + 1 - 2 * k, col)
+    pair = (row, (1 - l) * 4 + x)
+
+    barrier = pltpu.get_barrier_semaphore()
+    neighbours = (partner, *z_dev, *x_dev, sibling, pair)
+    for device in neighbours:
+        pl.semaphore_signal(barrier, inc=1, device_id=device, device_id_type=MESH)
+    pl.semaphore_wait(barrier, len(neighbours))
+
+    def halves(ref):
+        size = ref.shape[0] // 2
+        return [pl.ds(s * size, size) for s in range(2)]
+
+    half_a, half_b, half_i = halves(a_ref), halves(b_ref), halves(i_ref)
+    copies, to_sibling = [], []
+
+    def send(src, dst, device):
+        copy = pltpu.make_async_remote_copy(
+            src_ref=src,
+            dst_ref=dst,
+            send_sem=send_sem.at[len(copies)],
+            recv_sem=recv_sem.at[len(copies)],
+            device_id=device,
+            device_id_type=MESH,
+        )
+        copy.start()
+        copies.append(copy)
+        return copy
+
+    def pass_on(out, slot, part, device):
+        return send(out.at[slot, part], out.at[slot, part], device)
+
+    def share(out, slot):
+        to_sibling.append(send(out.at[slot], out.at[slot], sibling))
+
+    def forward(arrivals, out, slots, parts, devices):
+        sent = []
+        for d in range(2):
+            arrivals[d][d].wait_recv()
+            sent.append(pass_on(out, slots[d], parts[d], devices[d]))
+        arrivals[0][1].wait_recv()
+        arrivals[1][0].wait_recv()
+        return sent
+
+    a_y = [send(a_ref.at[p], out_a.at[row, p], partner) for p in half_a]
+    b_z = [[send(b_ref.at[p], out_b.at[row, p], z_dev[d]) for p in half_b] for d in range(2)]
+    i_x = [[send(i_ref.at[p], out_i.at[col, p], x_dev[d]) for p in half_i] for d in range(2)]
+    to_sibling.append(send(a_ref, out_a.at[row], sibling))
+    to_sibling.append(send(b_ref, out_b.at[row], sibling))
+    own = [
+        pltpu.make_async_copy(a_ref, out_a.at[row], own_sem.at[0]),
+        pltpu.make_async_copy(b_ref, out_b.at[row], own_sem.at[1]),
+        pltpu.make_async_copy(i_ref, out_i.at[col], own_sem.at[2]),
+    ]
+    for copy in own:
+        copy.start()
+
+    z_rows = (row_of(h, z + 3), row_of(h, z + 1))
+    far = row_of(h, z + 2)
+    x_cols = (l * 4 + (x + 3) % 4, l * 4 + (x + 1) % 4)
+    other = row_of(1 - h, z)
+    other_rows = (row_of(1 - h, z + 3), row_of(1 - h, z + 1))
+    other_far = row_of(1 - h, z + 2)
+    pair_col = (1 - l) * 4 + x
+    other_cols = ((1 - l) * 4 + (x + 3) % 4, (1 - l) * 4 + (x + 1) % 4)
+
+    b_zf = forward(b_z, out_b, z_rows, half_b, z_dev)
+    a_z = [[send(a_ref.at[p], out_a.at[row, p], z_dev[d]) for p in half_a] for d in range(2)]
+    for slot in z_rows:
+        share(out_b, slot)
+    a2_z = [[None, None], [None, None]]
+    for s in range(2):
+        a_y[s].wait_recv()
+        for d in range(2):
+            a2_z[d][s] = pass_on(out_a, other, half_a[s], z_dev[d])
+    share(out_a, other)
+    i_pair = send(i_ref, out_i.at[col], pair)
+    b_y = [send(b_ref, out_b.at[row], partner)]
+    for slot in z_rows:
+        b_y.append(send(out_b.at[slot], out_b.at[slot], partner))
+    i_xf = forward(i_x, out_i, x_cols, half_i, x_dev)
+    for d in range(2):
+        b_zf[d].wait_recv()
+    b_y.append(send(out_b.at[far], out_b.at[far], partner))
+    share(out_b, far)
+    a_zf = forward(a_z, out_a, z_rows, half_a, z_dev)
+    for slot in z_rows:
+        share(out_a, slot)
+    i_pair.wait_recv()
+    i2_x = [[pass_on(out_i, pair_col, p, x_dev[d]) for p in half_i] for d in range(2)]
+    for d in range(2):
+        a_zf[d].wait_recv()
+    share(out_a, far)
+    i2_xf = forward(i2_x, out_i, other_cols, half_i, x_dev)
+    a2_zf = forward(a2_z, out_a, other_rows, half_a, z_dev)
+    for slot in other_rows:
+        share(out_a, slot)
+    for slot, copy in zip((other, *other_rows, other_far), b_y):
+        copy.wait_recv()
+        share(out_b, slot)
+    for d in range(2):
+        a2_zf[d].wait_recv()
+    share(out_a, other_far)
+    for copy in (*i_xf, *i2_xf, *to_sibling):
+        copy.wait_recv()
+    for copy in own:
+        copy.wait()
+    assert len(copies) == gather_copies
+    for copy in copies:
+        copy.wait_send()
+
+
+def gather_all(a, b, i):
+    rows, cols = lax.axis_size("row"), lax.axis_size("col")
+    vmem = pl.BlockSpec(memory_space=pltpu.VMEM)
+    anywhere = pl.BlockSpec(memory_space=pl.ANY)
+    return pl.pallas_call(
+        gather_kernel,
+        in_specs=[vmem, vmem, vmem],
+        out_specs=[anywhere] * 3,
+        out_shape=[
+            jax.ShapeDtypeStruct((rows, *a.shape), a.dtype),
+            jax.ShapeDtypeStruct((rows, *b.shape), b.dtype),
+            jax.ShapeDtypeStruct((cols, *i.shape), i.dtype),
+        ],
+        scratch_shapes=[
+            pltpu.SemaphoreType.DMA((gather_copies,)),
+            pltpu.SemaphoreType.DMA((gather_copies,)),
+            pltpu.SemaphoreType.DMA((3,)),
+        ],
+        compiler_params=pltpu.CompilerParams(collective_id=0, has_side_effects=True),
+        name="gather_all",
+    )(a, b, i)
+
+
+def build_tiles(in_slots, tables, packed_a, packed_b, packed_i, pairs_max, blocks_dev, side):
+    rows, cols = packed_a.shape[0], packed_i.shape[0]
+    depth = packed_b.shape[1]
+    width = packed_i.shape[2]
+    spread, depth_out = cols * blocks_dev, rows * blocks_dev
     chunks = pairs_max // chunk_pairs
 
     def tile_chunk(s, *refs):
         last = jnp.maximum((refs[5][0] + chunk_pairs - 1) // chunk_pairs - 1, 0)
         return (jnp.clip(s - spread, 0, last), 0, 0)
 
-    def held(s, *refs):
-        return (0, 0, 0)
+    def coarse_at(s, slots, *refs):
+        return (slots[jnp.minimum(s, spread - 1)], 0, 0)
+
+    def over_in_at(s, *refs):
+        block = jnp.minimum(s, spread - 1)
+        return (block // blocks_dev, block % blocks_dev, 0)
 
     grid_spec = pltpu.PrefetchScalarGridSpec(
         num_scalar_prefetch=6,
         grid=(spread + chunks,),
         in_specs=[
-            pl.BlockSpec(
-                (points, 1, pairs_coarse, pairs_coarse),
-                lambda s, slots, *refs: (0, slots[jnp.minimum(s, spread - 1)], 0, 0),
-            ),
-            pl.BlockSpec(
-                (1, pairs_coarse, tile_side), lambda s, *refs: (jnp.minimum(s, spread - 1), 0, 0)
-            ),
-            pl.BlockSpec(over_out.shape, held),
-            pl.BlockSpec(fields.shape, held),
+            pl.BlockSpec((1, depth, depth), coarse_at),
+            pl.BlockSpec((1, depth, depth), coarse_at),
+            pl.BlockSpec((1, depth, side), over_in_at),
+            pl.BlockSpec(memory_space=pl.ANY),
+            pl.BlockSpec(memory_space=pl.ANY),
         ],
         out_specs=[
-            pl.BlockSpec((chunk_pairs, tile_side, 2 * tile_side), tile_chunk),
-            pl.BlockSpec((depth_out, tile_side, width), held),
+            pl.BlockSpec((chunk_pairs, side, 2 * side), tile_chunk),
+            pl.BlockSpec((depth_out, side, width), lambda s, *refs: (0, 0, 0)),
         ],
         scratch_shapes=[
-            pltpu.VMEM((spread * points, pairs_coarse, tile_side), jnp.bfloat16),
-            pltpu.VMEM((depth_out, tile_side, width), jnp.float32),
+            pltpu.VMEM((spread * 2, depth, side), jnp.bfloat16),
+            pltpu.VMEM((depth_out, side, width), jnp.float32),
+            pltpu.VMEM((rows, blocks_dev * side, depth), jnp.bfloat16),
+            pltpu.VMEM((cols + 1, blocks_dev * side, width), jnp.bfloat16),
+            pltpu.SemaphoreType.DMA((2,)),
         ],
     )
     return pl.pallas_call(
-        functools.partial(build_kernel, spread),
+        functools.partial(build_kernel, blocks_dev, spread),
         grid_spec=grid_spec,
         out_shape=[
-            jax.ShapeDtypeStruct((pairs_max, tile_side, 2 * tile_side), jnp.bfloat16),
-            jax.ShapeDtypeStruct((depth_out, tile_side, width), jnp.bfloat16),
-        ],
-        compiler_params=pltpu.CompilerParams(vmem_limit_bytes=52 * 1024 * 1024),
+            jax.ShapeDtypeStruct((pairs_max, side, 2 * side), jnp.bfloat16),
+            jax.ShapeDtypeStruct((depth_out, side, width), jnp.bfloat16),
+        ],
+        compiler_params=pltpu.CompilerParams(vmem_limit_bytes=40 * 1024 * 1024),
         name="build_tiles",
-    )(in_slots, *tables, coarse_strip, over_in, over_out, fields)
-
-
-def apply_tiles(tables, tiles, fields, depth_out):
-    pairs_max, tile_side, _ = tiles.shape
-    width = fields.shape[2]
+    )(in_slots, *tables, packed_a, packed_b, packed_i, packed_a, packed_i)
+
+
+def apply_tiles(tables, tiles, pieces, depth_out):
+    pairs_max, side, _ = tiles.shape
+    cols, rows_dev, width = pieces.shape
     out_idx, first, second, _, used = tables
 
     def tile_chunk(s, *refs):
@@ -215,19 +413,22 @@
         num_scalar_prefetch=4,
         grid=(pairs_max // chunk_pairs,),
         in_specs=[
-            pl.BlockSpec((chunk_pairs, tile_side, 2 * tile_side), tile_chunk),
-            pl.BlockSpec(fields.shape, held),
-        ],
-        out_specs=pl.BlockSpec((depth_out, tile_side, width), held),
-        scratch_shapes=[pltpu.VMEM((depth_out, tile_side, width), jnp.float32)],
+            pl.BlockSpec((chunk_pairs, side, 2 * side), tile_chunk),
+            pl.BlockSpec(pieces.shape, held),
+        ],
+        out_specs=pl.BlockSpec((depth_out, side, width), held),
+        scratch_shapes=[
+            pltpu.VMEM((depth_out, side, width), jnp.float32),
+            pltpu.VMEM((cols + 1, rows_dev, width), jnp.bfloat16),
+        ],
     )
     return pl.pallas_call(
         apply_kernel_body,
         grid_spec=grid_spec,
-        out_shape=jax.ShapeDtypeStruct((depth_out, tile_side, width), jnp.bfloat16),
+        out_shape=jax.ShapeDtypeStruct((depth_out, side, width), jnp.bfloat16),
         compiler_params=pltpu.CompilerParams(vmem_limit_bytes=32 * 1024 * 1024),
         name="apply_tiles",
-    )(out_idx, first, second, used, tiles, fields)
+    )(out_idx, first, second, used, tiles, pieces)
 
 
 def on_device(
@@ -256,33 +457,38 @@
         tile_codes[0], tile_count[0], depth_out, spread, out_points, pairs_max
     )
 
-    coarse_strip = lax.all_gather(coarse, "row", axis=1, tiled=True)
-    over_in = lax.all_gather(intersections, "col", axis=0, tiled=True)
-    over_out = lax.all_gather(jnp.swapaxes(intersections, 1, 2), "row", axis=0, tiled=True)
-
-    def gathered(field):
-        rounded = field.astype(jnp.bfloat16)
-        copies = jnp.broadcast_to(rounded, (cols_count, *rounded.shape))
-        pieces = lax.all_to_all(copies, "col", split_axis=0, concat_axis=0, tiled=True)
-        pieces = pieces.reshape(spread, tile_side, width_vec)
-        return jnp.pad(pieces, ((0, 1), (0, 0), (0, 0)))
+    start_vec = vectors.reshape(blocks_dev, tile_side, width_vec)
+    pair_energy = energies.reshape(blocks_dev, tile_side, 1)
+    across = jnp.swapaxes(intersections, 1, 2).reshape(-1, pairs_coarse)
+    packed_a, packed_b, packed_i = gather_all(
+        jnp.concatenate([coarse[0, 0], across], axis=0),
+        coarse[1, 0],
+        jnp.concatenate(
+            [intersections.reshape(-1, tile_side), vectors.astype(jnp.bfloat16)], axis=0
+        ),
+    )
 
     def summed(partial):
         parts = partial.reshape(rows_count, blocks_dev, tile_side, width_vec)
         arrived = lax.all_to_all(parts, "row", split_axis=0, concat_axis=0, tiled=True)
         return jnp.sum(arrived.astype(jnp.float32), axis=0)
 
-    start_vec = vectors.reshape(blocks_dev, tile_side, width_vec)
-    pair_energy = energies.reshape(blocks_dev, tile_side, 1)
-
     def shifted(field, kernel_part):
         return (pair_energy * field + kernel_part - spectrum_center * field) / spectrum_half
 
     tiles, partial = build_tiles(
-        in_slots, tables, coarse_strip, over_in, over_out, gathered(start_vec), pairs_max
+        in_slots, tables, packed_a, packed_b, packed_i, pairs_max, blocks_dev, tile_side
     )
     first_step = shifted(start_vec, summed(partial))
-    partial = apply_tiles(tables, tiles, gathered(first_step), depth_out)
+    rounded = first_step.astype(jnp.bfloat16).reshape(1, blocks_dev * tile_side, width_vec)
+    pieces = lax.all_to_all(
+        jnp.broadcast_to(rounded, (cols_count, *rounded.shape[1:])),
+        "col",
+        split_axis=0,
+        concat_axis=0,
+        tiled=True,
+    )
+    partial = apply_tiles(tables, tiles, pieces, depth_out)
     second_step = 2.0 * shifted(first_step, summed(partial)) - start_vec
     return (
         first_step.reshape(blocks_dev * tile_side, width_vec),

time: 409 us -> 266 us (0.65)
  waiting for transfers between devices: 240 us -> 22.7 us
  Pallas kernels: 50.7 us -> 154 us
  blocking collectives: 73.2 us -> 60 us
  between operations: 14.7 us -> 1.59 us
  starting transfers between devices: 15 us -> 5.42 us
  local copies, waits for them, and re-layouts: 9.73 us -> 14.3 us
    all_gather x3 -> x0, waiting for transfers between devices: 204 us -> none  [the longest x1 109 us: on_device(): coarse_strip = lax.all_gather(coarse, 'row', axis=1, tiled=True)]
    pallas_call x1 -> x2, Pallas kernels: 42.8 us -> 142 us  [the longest x1 91.1 us: gather_all(): pl.pallas_call(gather_kernel, in_specs=[vmem, vmem, vmem], out_specs=[any...]
    all_to_all x1 -> x0, waiting for transfers between devices: 12.1 us -> none  [gathered(): lax.all_to_all(copies, 'col', split_axis=0, concat_axis=0, tiled=True)]
    all_to_all x1, blocking collectives: 37.7 us -> 26.3 us  [summed(): lax.all_to_all(parts, 'row', split_axis=0, concat_axis=0, tiled=True)]
    all_to_all x1 -> x0, starting transfers between devices: 5.85 us -> none  [gathered(): lax.all_to_all(copies, 'col', split_axis=0, concat_axis=0, tiled=True)]
    pallas_call x1, Pallas kernels: 7.86 us -> 12.1 us  [apply_tiles(): pl.pallas_call(apply_kernel_body, grid_spec=grid_spec, out_shape=jax.Shap...]
    unnamed x13 -> x16, local copies, waits for them, and re-layouts: 7.4 us -> 11 us
  transfers between devices with their start and end apart: 5 -> 1, of which waited for: 5 -> 1; matrix products, arithmetic and copies ran while one was open for 2% -> 0% of each run, Pallas kernels for 0% -> 0%
where the time goes in v2:
time: 266 us
  Pallas kernels  154 us (58%)
  blocking collectives  60 us (23%)
  waiting for transfers between devices  22.7 us (9%)
  local copies, waits for them, and re-layouts  14.3 us (5%)
  other arithmetic  7.43 us (3%)
  starting transfers between devices  5.42 us (2%)
    pallas_call x1, Pallas kernels, gather_all(): pl.pallas_call(gather_kernel, in_specs=[vmem, vmem, vmem], out_specs=[any...  91.1 us
    pallas_call x1, Pallas kernels, build_tiles(): pl.pallas_call(functools.partial(build_kernel, blocks_dev, spread), grid_...  51.3 us
    all_to_all x1, blocking collectives, on_device(): lax.all_to_all(jnp.broadcast_to(rounded, (cols_count, *rounded.shape[1:])...  33.7 us
    all_to_all x1, blocking collectives, summed(): lax.all_to_all(parts, 'row', split_axis=0, concat_axis=0, tiled=True)  26.3 us
    all_to_all x1, waiting for transfers between devices, summed(): lax.all_to_all(parts, 'row', split_axis=0, concat_axis=0, tiled=True)  22.7 us
    pallas_call x1, Pallas kernels, apply_tiles(): pl.pallas_call(apply_kernel_body, grid_spec=grid_spec, out_shape=jax.Shap...  12.1 us
    unnamed x16, local copies, waits for them, and re-layouts  11 us
    all_to_all x1, starting transfers between devices, summed(): lax.all_to_all(parts, 'row', split_axis=0, concat_axis=0, tiled=True)  5.42 us
  transfers between devices with their start and end apart: 1, of which 1 were waited for; matrix products, arithmetic and copies ran while one was open for 0% of the time, Pallas kernels for 0%

profile of v2, /device:TPU:1, one launch (start us, length us, event | category | flops | bytes accessed | tf_op | source)
XLA Modules:
  0.0 265.9 jit_solution(10550165772015032419)
XLA Ops:
  0.6 0.0 copy-start.4
  0.6 0.0 copy-start.3
  0.6 0.0 copy-start.6
  1.4 1.0 fusion.1
  2.4 0.1 reshape.187
  2.5 0.1 copy.12
  2.6 0.1 reduce_sum.105
  2.7 0.7 fusion.22
  3.3 0.1 select_reduce_fusion.5
  3.5 0.2 select_reduce_fusion.1
  3.6 0.1 copy.13
  3.7 0.1 add.134
  3.8 0.3 select_reduce_fusion
  4.2 0.2 gt.19
  4.3 0.1 max.7
  4.5 0.1 slice_reduce_fusion.2
  4.6 0.2 fusion.9
  4.8 0.1 fusion.7
  4.9 0.2 slice_reduce_fusion
  5.2 2.1 slice_bitcast_fusion
  7.2 0.0 copy-start.7
  7.3 0.0 copy-done.4
  7.3 0.2 copy.14
  7.4 0.0 copy-done.3
  7.5 0.0 copy-done.6
  7.5 0.2 select_reduce_fusion.2
  7.7 0.2 select_reduce_fusion.4
  7.9 0.1 reduce.1
  8.0 0.1 select_reduce_fusion.3.point_idx
  8.1 1.0 pad_maximum_fusion.a_ref
  9.1 0.8 pad_maximum_fusion.1.i_ref
  9.9 0.0 copy-done.7
  9.9 0.1 select_reduce_fusion.6.slots_ref
  10.0 91.1 %gather_all.1 = (bf16[16,896,512]{2,1,0:T(8,128)(2,1)}, bf16[16,512,512]{2,1,0:T(8,128)(2,1)}, bf16[8,1920,128]{2,1,0:T(8,128)(2,1)}) custom-call(bf16[896,512]{1,0:T(8,128)(2,1)} %pad_maximum_fusion.a_ref, bf16[512,512]{1,0:T(8,128)(2,1)} %get-tuple-element.21.b_ref, bf16[1920,128]{1,0:T(8,128)(2,1)} %pad_maximum_fusion.1.i_ref), custom_call_target="tpu_custom_call" | custom-call | tf_op jit(solution)/shard_map/gather_all/pallas_call | solution.py:329
  101.1 0.0 copy-start.1
  101.2 2.1 copy-done.1
  103.3 0.0 copy-start.2
  103.3 3.4 %copy-done.2 = bf16[16,512,512]{2,1,0:T(8,128)(2,1)S(1)} copy-done((bf16[16,512,512]{2,1,0:T(8,128)(2,1)S(1)}, bf16[16,512,512]{2,1,0:T(8,128)(2,1)}, u32[]{:S(2)}) %copy-start.2) | copy-done | bytes 8388632
  106.6 51.3 %build_tiles.1 = (bf16[240,128,256]{2,1,0:T(8,128)(2,1)}, bf16[48,128,128]{2,1,0:T(8,128)(2,1)S(1)}) custom-call(s32[24]{0:T(128)S(1)} %select_reduce_fusion.6.slots_ref, s32[240]{0:T(256)S(1)} %fusion.12.out_ref_idx, s32[240]{0:T(256)S(1)} %get-tuple-element.15.first_idx, s32[240]{0:T(256)S(1)} %get-tuple-element.14.second_idx, ...), custom_call_target="tpu_custom_call" | custom-call | tf_op jit(solution)/shard_map/build_tiles/pallas_call | solution.py:388
  157.9 0.0 copy-start.5
  158.0 26.3 %all_to_all.15 = bf16[16,3,128,128]{3,2,1,0:T(8,128)(2,1)S(1)} all-to-all(bf16[16,3,128,128]{3,2,1,0:T(8,128)(2,1)S(1)} %bitcast.30), channel_id=1, replica_groups=mesh['row'=16,'col'=8] {'row'}, dimensions={0} | all-to-all | bytes 3145728 | tf_op jit(solution)/shard_map/all_to_all | solution.py:473
  184.2 0.3 convert_reduce_fusion.1
  184.5 0.0 copy-done.5
  184.5 0.8 fusion.20
  185.3 0.1 broadcast_in_dim.149
  185.4 33.7 %all_to_all.16.pieces_ref = bf16[8,384,128]{2,1,0:T(8,128)(2,1)S(1)} all-to-all(bf16[8,384,128]{2,1,0:T(8,128)(2,1)S(1)} %broadcast_in_dim.149), channel_id=1, replica_groups=mesh['row'=16,'col'=8] {'col'}, dimensions={0} | all-to-all | bytes 1572864 | tf_op jit(solution)/shard_map/all_to_all | solution.py:484
  219.1 0.0 copy-start
  219.1 5.5 %copy-done = bf16[240,128,256]{2,1,0:T(8,128)(2,1)S(1)} copy-done((bf16[240,128,256]{2,1,0:T(8,128)(2,1)S(1)}, bf16[240,128,256]{2,1,0:T(8,128)(2,1)}, u32[]{:S(2)}) %copy-start) | copy-done | bytes 15728664
  224.6 12.1 %apply_tiles.1 = bf16[48,128,128]{2,1,0:T(8,128)(2,1)} custom-call(s32[240]{0:T(256)S(1)} %fusion.12.out_ref_idx, s32[240]{0:T(256)S(1)} %get-tuple-element.15.first_idx, s32[240]{0:T(256)S(1)} %get-tuple-element.14.second_idx, s32[1]{0:T(128)} %bitcast.2.used_ref, bf16[240,128,256]{2,1,0:T(8,128)(2,1)S(1)} %copy-done, ...), custom_call_target="tpu_custom_call" | custom-call | tf_op jit(solution)/shard_map/apply_tiles/pallas_call | solution.py:425
  236.7 5.4 %all-to-all-start.2 = ((bf16[16,3,128,128]{3,2,1,0:T(8,128)(2,1)}), bf16[16,3,128,128]{3,2,1,0:T(8,128)(2,1)S(1)}, u32[]{:S(2)}, u32[]{:S(2)}) async-start(bf16[16,3,128,128]{3,2,1,0:T(8,128)(2,1)} %bitcast.10), calls=%async_computation.2 | async-start | bytes 3145728 | tf_op jit(solution)/shard_map/all_to_all | solution.py:473
  242.1 22.7 %all-to-all-done.2 = bf16[16,3,128,128]{3,2,1,0:T(8,128)(2,1)S(1)} async-done(((bf16[16,3,128,128]{3,2,1,0:T(8,128)(2,1)}), bf16[16,3,128,128]{3,2,1,0:T(8,128)(2,1)S(1)}, u32[]{:S(2)}, u32[]{:S(2)}) %all-to-all-start.2) | async-done | bytes 1572896 | tf_op jit(solution)/shard_map/all_to_all | solution.py:473
  264.8 0.3 convert_reduce_fusion
  265.1 0.9 fusion.4
  (14 shorter events, 0.1 us)
Async XLA Ops:
  0.6 6.6 %copy-start.4 = (bf16[3,512,128]{2,1,0:T(8,128)(2,1)S(1)}, bf16[3,512,128]{2,1,0:T(8,128)(2,1)}, u32[]{:S(2)}) copy-start(bf16[3,512,128]{2,1,0:T(8,128)(2,1)} %param.10) | copy-start | bytes 1179652
  0.6 6.8 %copy-start.3 = (f32[384,128]{1,0:T(8,128)S(1)}, f32[384,128]{1,0:T(8,128)}, u32[]{:S(2)}) copy-start(f32[384,128]{1,0:T(8,128)} %param.8) | copy-start | bytes 589828
  0.6 6.8 %copy-start.6 = (s32[384]{0:T(512)S(1)}, s32[384]{0:T(512)}, u32[]{:S(2)}) copy-start(s32[384]{0:T(512)} %param.12) | copy-start | bytes 4612
  7.2 2.7 %copy-start.7 = (s32[16]{0:T(128)S(1)}, s32[16]{0:T(128)}, u32[]{:S(2)}) copy-start(s32[16]{0:T(128)} %param.13) | copy-start | bytes 196
  101.1 2.1 copy-start.1
  103.3 3.4 %copy-start.2 = (bf16[16,512,512]{2,1,0:T(8,128)(2,1)S(1)}, bf16[16,512,512]{2,1,0:T(8,128)(2,1)}, u32[]{:S(2)}) copy-start(bf16[16,512,512]{2,1,0:T(8,128)(2,1)} %get-tuple-element.8.coarse_b_ref) | copy-start | bytes 25165828
  157.9 26.6 %copy-start.5 = (f32[384]{0:T(512)S(1)}, f32[384]{0:T(512)}, u32[]{:S(2)}) copy-start(f32[384]{0:T(512)} %param.9) | copy-start | bytes 4612
  219.1 5.5 %copy-start = (bf16[240,128,256]{2,1,0:T(8,128)(2,1)S(1)}, bf16[240,128,256]{2,1,0:T(8,128)(2,1)}, u32[]{:S(2)}) copy-start(bf16[240,128,256]{2,1,0:T(8,128)(2,1)} %get-tuple-element.11.tiles_ref) | copy-start | bytes 47185924
  236.7 28.1 %all-to-all-start.2 = ((bf16[16,3,128,128]{3,2,1,0:T(8,128)(2,1)}), bf16[16,3,128,128]{3,2,1,0:T(8,128)(2,1)S(1)}, u32[]{:S(2)}, u32[]{:S(2)}) async-start(bf16[16,3,128,128]{3,2,1,0:T(8,128)(2,1)} %bitcast.10), calls=%async_computation.2 | async-start | bytes 3145728 | tf_op jit(solution)/shard_map/all_to_all | solution.py:473

commit v3 on v2

--- a/solution.py
+++ b/solution.py
@@ -10,8 +10,9 @@
 spectrum_center = 2.0
 spectrum_half = 3.0
 chunk_pairs = 16
-unroll_pairs = 4
+unroll_pairs = 8
 gather_copies = 53
+block_parts = 3
 MESH = pl.DeviceIdType.MESH
 
 
@@ -76,9 +77,8 @@
     packed_a_ref,
     packed_i_ref,
     tiles_ref,
-    partial_ref,
+    total_ref,
     projected_ref,
-    total_ref,
     over_out_ref,
     fields_ref,
     sems,
@@ -144,10 +144,6 @@
 
         lax.fori_loop(0, chunk_pairs // unroll_pairs, group, 0)
 
-    @pl.when(step == pl.num_programs(0) - 1)
-    def _():
-        partial_ref[...] = total_ref[...].astype(partial_ref.dtype)
-
 
 def apply_kernel_body(
     out_ref_idx,
@@ -156,7 +152,6 @@
     used_ref,
     tiles_ref,
     pieces_ref,
-    partial_ref,
     total_ref,
     fields_ref,
 ):
@@ -175,8 +170,8 @@
     def _():
         def group(g, carry):
             adds = []
-            for k in range(unroll_pairs):
-                local = g * unroll_pairs + k
+            for k in range(chunk_pairs):
+                local = g * chunk_pairs + k
                 pair = start + local
                 adds.append(
                     add_pair(
@@ -192,11 +187,7 @@
                 ref[block] += product
             return carry
 
-        lax.fori_loop(0, chunk_pairs // unroll_pairs, group, 0)
-
-    @pl.when(step == pl.num_programs(0) - 1)
-    def _():
-        partial_ref[...] = total_ref[...].astype(partial_ref.dtype)
+        lax.fori_loop(0, chunk_pairs // chunk_pairs, group, 0)
 
 
 def gather_kernel(a_ref, b_ref, i_ref, out_a, out_b, out_i, send_sem, recv_sem, own_sem):
@@ -345,6 +336,122 @@
     )(a, b, i)
 
 
+def exchange_kernel(spread_on, partial_ref, linear_ref, *refs):
+    if spread_on:
+        out_ref, pieces_ref, from_core, mine, landed, rounded, send_sem, recv_sem, own_sem = refs
+    else:
+        out_ref, from_core, mine, landed, send_sem, recv_sem = refs
+    row, col = lax.axis_index("row"), lax.axis_index("col")
+    h, z, k = row // 8, row // 2 % 4, row % 2
+    l, x = col // 4, col % 4
+    turns = ((1, 2), (1, 1), (1, 3), (0, 2), (1, 0), (0, 1), (0, 3), (0, 0))
+
+    def row_of(turn, kk):
+        return ((h + turn[0]) % 2 * 4 + (z + turn[1]) % 4) * 2 + kk
+
+    def col_of(turn):
+        return (l + turn[0]) % 2 * 4 + (x + turn[1]) % 4
+
+    sibling = (row + 1 - 2 * k, col)
+    neighbours = [sibling] + [(row_of(turn, k), col) for turn in turns[:-1]]
+    if spread_on:
+        neighbours += [(row, col_of(turn)) for turn in turns[:-1]]
+    barrier = pltpu.get_barrier_semaphore()
+    for device in neighbours:
+        pl.semaphore_signal(barrier, inc=1, device_id=device, device_id_type=MESH)
+    pl.semaphore_wait(barrier, len(neighbours))
+    copies = []
+
+    def send(src, dst, device):
+        copy = pltpu.make_async_remote_copy(
+            src_ref=src,
+            dst_ref=dst,
+            send_sem=send_sem.at[len(copies)],
+            recv_sem=recv_sem.at[len(copies)],
+            device_id=device,
+            device_id_type=MESH,
+        )
+        copy.start()
+        copies.append(copy)
+        return copy
+
+    peers = len(turns) - 1
+    side = partial_ref.shape[1] // block_parts
+    parts = [pl.ds(t * side, side) for t in range(block_parts)]
+    crossed = [
+        send(partial_ref.at[row_of(turn, 1 - k)], from_core.at[i], sibling)
+        for i, turn in enumerate(turns)
+    ]
+    arrivals = []
+
+    def send_on(i):
+        device = (row_of(turns[i], k), col)
+        arrivals.append([send(mine.at[i, p], landed.at[i, p], device) for p in parts])
+
+    for i in range(peers):
+        crossed[i].wait_recv()
+        mine[i] = (partial_ref[row_of(turns[i], k)] + from_core[i]).astype(mine.dtype)
+        if i > 0:
+            send_on(i - 1)
+    crossed[peers].wait_recv()
+    send_on(peers - 1)
+    spreads, own = [], []
+    for t, p in enumerate(parts):
+        total = partial_ref[row, p] + from_core[peers, p]
+        for i in range(peers - 1, -1, -1):
+            arrivals[i][t].wait_recv()
+            total += landed[i, p].astype(jnp.float32)
+        if spread_on:
+            total = (linear_ref[p] + total) / spectrum_half
+            rounded[p] = total.astype(rounded.dtype)
+            out_ref[p] = total
+            for turn in turns[:-1]:
+                device = (row, col_of(turn))
+                spreads.append(send(rounded.at[p], pieces_ref.at[col, p], device))
+            own.append(pltpu.make_async_copy(rounded.at[p], pieces_ref.at[col, p], own_sem.at[t]))
+            own[-1].start()
+        else:
+            out_ref[p] = total
+    for copy in spreads:
+        copy.wait_recv()
+    for copy in own:
+        copy.wait()
+    for copy in copies:
+        copy.wait_send()
+
+
+def exchange(partial, linear, spread_on):
+    rows, rows_dev, width = partial.shape
+    cols = lax.axis_size("col")
+    count = 8 + 7 * block_parts * (2 if spread_on else 1)
+    vmem = pl.BlockSpec(memory_space=pltpu.VMEM)
+    block = jax.ShapeDtypeStruct((rows_dev, width), jnp.float32)
+    scratch = [
+        pltpu.VMEM((8, rows_dev, width), jnp.float32),
+        pltpu.VMEM((7, rows_dev, width), jnp.bfloat16),
+        pltpu.VMEM((7, rows_dev, width), jnp.bfloat16),
+    ]
+    sems = [pltpu.SemaphoreType.DMA((count,)), pltpu.SemaphoreType.DMA((count,))]
+    if spread_on:
+        out_shape = [block, jax.ShapeDtypeStruct((cols, rows_dev, width), jnp.bfloat16)]
+        out_specs = [vmem, pl.BlockSpec(memory_space=pl.ANY)]
+        scratch.append(pltpu.VMEM((rows_dev, width), jnp.bfloat16))
+        sems.append(pltpu.SemaphoreType.DMA((block_parts,)))
+    else:
+        out_shape, out_specs = block, vmem
+    return pl.pallas_call(
+        functools.partial(exchange_kernel, spread_on),
+        in_specs=[vmem, vmem],
+        out_specs=out_specs,
+        out_shape=out_shape,
+        scratch_shapes=scratch + sems,
+        compiler_params=pltpu.CompilerParams(
+            collective_id=1 if spread_on else 2, has_side_effects=True
+        ),
+        name="exchange_spread" if spread_on else "exchange",
+    )(partial, linear)
+
+
 def build_tiles(in_slots, tables, packed_a, packed_b, packed_i, pairs_max, blocks_dev, side):
     rows, cols = packed_a.shape[0], packed_i.shape[0]
     depth = packed_b.shape[1]
@@ -379,7 +486,6 @@
         ],
         scratch_shapes=[
             pltpu.VMEM((spread * 2, depth, side), jnp.bfloat16),
-            pltpu.VMEM((depth_out, side, width), jnp.float32),
             pltpu.VMEM((rows, blocks_dev * side, depth), jnp.bfloat16),
             pltpu.VMEM((cols + 1, blocks_dev * side, width), jnp.bfloat16),
             pltpu.SemaphoreType.DMA((2,)),
@@ -390,9 +496,9 @@
         grid_spec=grid_spec,
         out_shape=[
             jax.ShapeDtypeStruct((pairs_max, side, 2 * side), jnp.bfloat16),
-            jax.ShapeDtypeStruct((depth_out, side, width), jnp.bfloat16),
-        ],
-        compiler_params=pltpu.CompilerParams(vmem_limit_bytes=40 * 1024 * 1024),
+            jax.ShapeDtypeStruct((depth_out, side, width), jnp.float32),
+        ],
+        compiler_params=pltpu.CompilerParams(vmem_limit_bytes=60 * 1024 * 1024),
         name="build_tiles",
     )(in_slots, *tables, packed_a, packed_b, packed_i, packed_a, packed_i)
 
@@ -418,15 +524,14 @@
         ],
         out_specs=pl.BlockSpec((depth_out, side, width), held),
         scratch_shapes=[
-            pltpu.VMEM((depth_out, side, width), jnp.float32),
             pltpu.VMEM((cols + 1, rows_dev, width), jnp.bfloat16),
         ],
     )
     return pl.pallas_call(
         apply_kernel_body,
         grid_spec=grid_spec,
-        out_shape=jax.ShapeDtypeStruct((depth_out, side, width), jnp.bfloat16),
-        compiler_params=pltpu.CompilerParams(vmem_limit_bytes=32 * 1024 * 1024),
+        out_shape=jax.ShapeDtypeStruct((depth_out, side, width), jnp.float32),
+        compiler_params=pltpu.CompilerParams(vmem_limit_bytes=60 * 1024 * 1024),
         name="apply_tiles",
     )(out_idx, first, second, used, tiles, pieces)
 
@@ -457,8 +562,7 @@
         tile_codes[0], tile_count[0], depth_out, spread, out_points, pairs_max
     )
 
-    start_vec = vectors.reshape(blocks_dev, tile_side, width_vec)
-    pair_energy = energies.reshape(blocks_dev, tile_side, 1)
+    pair_energy = energies.reshape(-1, 1)
     across = jnp.swapaxes(intersections, 1, 2).reshape(-1, pairs_coarse)
     packed_a, packed_b, packed_i = gather_all(
         jnp.concatenate([coarse[0, 0], across], axis=0),
@@ -468,32 +572,20 @@
         ),
     )
 
-    def summed(partial):
-        parts = partial.reshape(rows_count, blocks_dev, tile_side, width_vec)
-        arrived = lax.all_to_all(parts, "row", split_axis=0, concat_axis=0, tiled=True)
-        return jnp.sum(arrived.astype(jnp.float32), axis=0)
-
-    def shifted(field, kernel_part):
-        return (pair_energy * field + kernel_part - spectrum_center * field) / spectrum_half
+    def linear(field):
+        return pair_energy * field - spectrum_center * field
+
+    def by_row(partial):
+        return partial.reshape(rows_count, -1, width_vec)
 
     tiles, partial = build_tiles(
         in_slots, tables, packed_a, packed_b, packed_i, pairs_max, blocks_dev, tile_side
     )
-    first_step = shifted(start_vec, summed(partial))
-    rounded = first_step.astype(jnp.bfloat16).reshape(1, blocks_dev * tile_side, width_vec)
-    pieces = lax.all_to_all(
-        jnp.broadcast_to(rounded, (cols_count, *rounded.shape[1:])),
-        "col",
-        split_axis=0,
-        concat_axis=0,
-        tiled=True,
-    )
+    first_step, pieces = exchange(by_row(partial), linear(vectors), True)
     partial = apply_tiles(tables, tiles, pieces, depth_out)
-    second_step = 2.0 * shifted(first_step, summed(partial)) - start_vec
-    return (
-        first_step.reshape(blocks_dev * tile_side, width_vec),
-        second_step.reshape(blocks_dev * tile_side, width_vec),
-    )
+    kernel_part = exchange(by_row(partial), vectors, False)
+    second_step = 2.0 * ((linear(first_step) + kernel_part) / spectrum_half) - vectors
+    return first_step, second_step
 
 
 def solution(mesh):

time: 266 us -> 246 us (0.925)
  Pallas kernels: 154 us -> 227 us
  blocking collectives: 60 us -> 0 us
  waiting for transfers between devices: 22.7 us -> 0 us
  local copies, waits for them, and re-layouts: 14.3 us -> 4.23 us
  starting transfers between devices: 5.42 us -> 0 us
  other arithmetic: 7.43 us -> 12.5 us
    pallas_call x0 -> x2, Pallas kernels: none -> 83.9 us  [exchange(): pl.pallas_call(functools.partial(exchange_kernel, spread_on), in_specs=[v...]
    all_to_all x2 -> x0, blocking collectives: 60 us -> none  [the longest x1 33.7 us: on_device(): lax.all_to_all(jnp.broadcast_to(rounded, (cols_count, *rounded.shape[1:])...]
    all_to_all x1 -> x0, waiting for transfers between devices: 22.7 us -> none  [summed(): lax.all_to_all(parts, 'row', split_axis=0, concat_axis=0, tiled=True)]
    unnamed x16 -> x11, local copies, waits for them, and re-layouts: 11 us -> 0.7 us
    pallas_call x1, Pallas kernels: 51.3 us -> 42.6 us  [build_tiles(): pl.pallas_call(functools.partial(build_kernel, blocks_dev, spread), grid_...]
    all_to_all x1 -> x0, starting transfers between devices: 5.42 us -> none  [summed(): lax.all_to_all(parts, 'row', split_axis=0, concat_axis=0, tiled=True)]
    reduce_sum x4, other arithmetic: 0.54 us -> 3.69 us  [lookup(): return jnp.sum(jnp.where(matches, values_table[None, :], 0), axis=1)]
    pallas_call x1, Pallas kernels: 12.1 us -> 9.15 us  [apply_tiles(): pl.pallas_call(apply_kernel_body, grid_spec=grid_spec, out_shape=jax.Shap...]
  transfers between devices with their start and end apart: 1 -> 0, of which waited for: 1 -> 0; matrix products, arithmetic and copies ran while one was open for 0% -> 0% of each run, Pallas kernels for 0% -> 0%
where the time goes in v3:
time: 246 us; the launch traced here: 245 us
  Pallas kernels  227 us (92%)
  other arithmetic  12.5 us (5%)
  local copies, waits for them, and re-layouts  4.23 us (2%)
    pallas_call x1, Pallas kernels, gather_all(): pl.pallas_call(gather_kernel, in_specs=[vmem, vmem, vmem], out_specs=[any...  91 us
    pallas_call x2, Pallas kernels, exchange(): pl.pallas_call(functools.partial(exchange_kernel, spread_on), in_specs=[v...  83.9 us
    pallas_call x1, Pallas kernels, build_tiles(): pl.pallas_call(functools.partial(build_kernel, blocks_dev, spread), grid_...  42.6 us
    pallas_call x1, Pallas kernels, apply_tiles(): pl.pallas_call(apply_kernel_body, grid_spec=grid_spec, out_shape=jax.Shap...  9.15 us

profile of v3, /device:TPU:1, one launch (start us, length us, event | category | flops | bytes accessed | tf_op | source)
XLA Modules:
  0.0 245.0 jit_solution(5580403112242241320)
XLA Ops:
  0.6 0.0 copy-start.1
  0.6 0.0 copy-start.2
  1.4 0.9 select_reduce_fusion.4
  2.3 0.9 select_reduce_fusion.2
  3.2 1.3 select_reduce_fusion.6.slots_ref
  4.5 1.0 fusion.1
  5.6 0.1 reshape.163
  5.7 0.1 reduce_sum.83
  5.8 0.1 copy.12
  5.8 0.2 select_reduce_fusion.1
  6.0 0.7 fusion.15
  6.7 0.1 select_reduce_fusion.5
  6.8 0.1 copy.13
  6.9 0.1 add.126
  7.0 0.3 select_reduce_fusion
  7.3 0.2 gt.19
  7.5 0.1 slice_reduce_fusion.2
  7.6 0.1 max.7
  7.8 0.2 fusion.4
  8.0 0.1 fusion.2
  8.1 0.8 slice_reduce_fusion
  8.8 0.7 select_reduce_fusion.3.point_idx
  9.5 0.1 reduce.1
  9.6 0.6 fusion.7.out_ref_idx
  10.2 1.8 multiply_subtract_fusion.1
  12.0 1.2 copy.14
  13.2 0.0 copy-done.1
  13.2 0.8 pad_maximum_fusion.1.i_ref
  14.0 0.0 copy-done.2
  14.0 0.9 slice_bitcast_fusion
  14.9 1.0 pad_maximum_fusion.a_ref
  15.8 91.0 %gather_all.1 = (bf16[16,896,512]{2,1,0:T(8,128)(2,1)}, bf16[16,512,512]{2,1,0:T(8,128)(2,1)}, bf16[8,1920,128]{2,1,0:T(8,128)(2,1)}) custom-call(bf16[896,512]{1,0:T(8,128)(2,1)} %pad_maximum_fusion.a_ref, bf16[512,512]{1,0:T(8,128)(2,1)} %get-tuple-element.23.b_ref, bf16[1920,128]{1,0:T(8,128)(2,1)} %pad_maximum_fusion.1.i_ref), custom_call_target="tpu_custom_call" | custom-call | tf_op jit(solution)/shard_map/gather_all/pallas_call | solution.py:320
  106.9 42.6 %build_tiles.1 = (bf16[240,128,256]{2,1,0:T(8,128)(2,1)}, f32[48,128,128]{2,1,0:T(8,128)}) custom-call(s32[24]{0:T(128)} %select_reduce_fusion.6.slots_ref, s32[240]{0:T(256)} %fusion.7.out_ref_idx, s32[240]{0:T(256)} %get-tuple-element.19.first_idx, s32[240]{0:T(256)} %get-tuple-element.18.second_idx, s32[240]{0:T(256)} %select_reduce_fusion.3.point_idx, ...), custom_call_target="tpu_custom_call" | custom-call | tf_op jit(solution)/shard_map/build_tiles/pallas_call | solution.py:494
  149.5 55.6 %exchange_spread.1 = (f32[384,128]{1,0:T(8,128)}, bf16[8,384,128]{2,1,0:T(8,128)(2,1)}) custom-call(f32[16,384,128]{2,1,0:T(8,128)} %bitcast.14, f32[384,128]{1,0:T(8,128)} %get-tuple-element.25.linear_ref), custom_call_target="tpu_custom_call" | custom-call | tf_op jit(solution)/shard_map/exchange_spread/pallas_call | solution.py:442
  205.2 9.1 %apply_tiles.1 = f32[48,128,128]{2,1,0:T(8,128)} custom-call(s32[240]{0:T(256)} %fusion.7.out_ref_idx, s32[240]{0:T(256)} %get-tuple-element.19.first_idx, s32[240]{0:T(256)} %get-tuple-element.18.second_idx, s32[1]{0:T(128)} %bitcast.2.used_ref, bf16[240,128,256]{2,1,0:T(8,128)(2,1)} %get-tuple-element.14.tiles_ref, ...), custom_call_target="tpu_custom_call" | custom-call | tf_op jit(solution)/shard_map/apply_tiles/pallas_call | solution.py:530
  214.3 0.0 copy-start
  214.3 0.0 copy-start.3
  214.3 0.0 copy-start.4
  214.3 28.3 %exchange.1 = f32[384,128]{1,0:T(8,128)} custom-call(f32[16,384,128]{2,1,0:T(8,128)} %bitcast.13, f32[384,128]{1,0:T(8,128)} %linear_ref.1), custom_call_target="tpu_custom_call" | custom-call | tf_op jit(solution)/shard_map/exchange/pallas_call | solution.py:442
  242.6 0.0 copy-done
  242.6 0.0 copy-done.3
  242.6 0.0 copy-done.4
  242.6 1.7 multiply_subtract_fusion
  244.4 0.7 copy.17
  (11 shorter events, 0.1 us)
Async XLA Ops:
  0.6 12.5 %copy-start.1 = (bf16[3,512,128]{2,1,0:T(8,128)(2,1)S(1)}, bf16[3,512,128]{2,1,0:T(8,128)(2,1)}, u32[]{:S(2)}) copy-start(bf16[3,512,128]{2,1,0:T(8,128)(2,1)} %param.10) | copy-start | bytes 1179652
  0.6 13.4 %copy-start.2 = (bf16[2,1,512,512]{3,2,1,0:T(8,128)(2,1)S(1)}, bf16[2,1,512,512]{3,2,1,0:T(8,128)(2,1)}, u32[]{:S(2)}) copy-start(bf16[2,1,512,512]{3,2,1,0:T(8,128)(2,1)} %param.11) | copy-start | bytes 3145732
  214.3 28.3 %copy-start = (f32[384,128]{1,0:T(8,128)S(1)}, f32[384,128]{1,0:T(8,128)}, u32[]{:S(2)}) copy-start(f32[384,128]{1,0:T(8,128)} %linear_ref.1) | copy-start | bytes 589828
  214.3 28.3 %copy-start.3 = (f32[384,128]{1,0:T(8,128)S(1)}, f32[384,128]{1,0:T(8,128)}, u32[]{:S(2)}) copy-start(f32[384,128]{1,0:T(8,128)} %get-tuple-element.31) | copy-start | bytes 589828
  214.3 28.3 %copy-start.4 = (f32[384]{0:T(512)S(1)}, f32[384]{0:T(512)}, u32[]{:S(2)}) copy-start(f32[384]{0:T(512)} %param.9) | copy-start | bytes 4612

commit v4 on v3

--- a/solution.py
+++ b/solution.py
@@ -9,8 +9,9 @@
 
 spectrum_center = 2.0
 spectrum_half = 3.0
-chunk_pairs = 16
-unroll_pairs = 8
+unroll_blocks = 4
+apply_group = 4
+ring = 6
 gather_copies = 53
 block_parts = 3
 MESH = pl.DeviceIdType.MESH
@@ -35,17 +36,10 @@
         jnp.where(index_in[None, None, :] < index_in[None, :, None], mask[:, None, :], 0), axis=2
     )
     place = jnp.where(mask > 0, 2 * base[:, None] + rank, -1).reshape(-1)
+    product = (index_in[None, :] * 2 + points[:, None]).reshape(-1)
     spots = jnp.arange(2 * pairs_max, dtype=jnp.int32)
-    found = jnp.sum(
-        jnp.where(spots[:, None] == place[None, :], all_codes[None, :] + 1, 0), axis=1
-    )
-    found = found.reshape(pairs_max, 2)
-    live = found > 0
-    code = jnp.maximum(found - 1, 0)
-    out_idx = jnp.where(live[:, 0], code[:, 0] // spread, depth_out - 1)
-    in_idx = jnp.where(live, code % spread, spread)
-    point = lookup(points, out_idx)
-    return out_idx, in_idx[:, 0], in_idx[:, 1], point, jnp.sum(pairs).reshape(1)
+    found = jnp.sum(jnp.where(spots[:, None] == place[None, :], product[None, :] + 1, 0), axis=1)
+    return jnp.where(found > 0, found - 1, 2 * spread), base, pairs
 
 
 def block_of(ref, block, blocks_dev, side):
@@ -53,141 +47,176 @@
     return ref[block // blocks_dev, rows, :]
 
 
-def add_pair(total_ref, fields_ref, tile, block, first, second):
-    blocks_dev = fields_ref.shape[1] // total_ref.shape[1]
-    side = total_ref.shape[1]
-    both = jnp.concatenate(
-        [block_of(fields_ref, place, blocks_dev, side) for place in (first, second)], axis=0
-    )
-    return total_ref, block, jnp.dot(tile, both, preferred_element_type=jnp.float32)
+def sum_products(members_ref, base_ref, pairs_ref, products_ref, sums_ref, over_out_ref, out_ref):
+    depth_out, side, width = out_ref.shape
+    blocks_dev = over_out_ref.shape[1] // side
+    depth = products_ref.shape[1]
+    half = depth // 2
+
+    def add_up(q, carry):
+        start = base_ref[q]
+        stop = start + pairs_ref[q]
+        for c in range(2):
+            rows = pl.ds(c * half, half)
+
+            def add(pair, total):
+                first, second = members_ref[2 * pair], members_ref[2 * pair + 1]
+                return total + (products_ref[first, rows, :] + products_ref[second, rows, :])
+
+            total = lax.fori_loop(start, stop, add, jnp.zeros((half, width), jnp.float32))
+            sums_ref[q, rows, :] = total.astype(sums_ref.dtype)
+        return carry
+
+    lax.fori_loop(0, depth_out, add_up, 0)
+
+    def finish(group, carry):
+        for u in range(unroll_blocks):
+            q = group * unroll_blocks + u
+            out_ref[q] = jnp.dot(
+                block_of(over_out_ref, q, blocks_dev, side),
+                sums_ref[q],
+                preferred_element_type=jnp.float32,
+            )
+        return carry
+
+    lax.fori_loop(0, depth_out // unroll_blocks, finish, 0)
 
 
 def build_kernel(
     blocks_dev,
     spread,
     slots_ref,
-    out_ref_idx,
-    first_idx,
-    second_idx,
-    point_idx,
-    used_ref,
-    coarse_a_ref,
-    coarse_b_ref,
+    members_ref,
+    base_ref,
+    pairs_ref,
+    packed_a_ref,
+    packed_b_ref,
+    packed_i_ref,
+    projected_ref,
+    out_ref,
+    products_ref,
+    sums_ref,
+    over_out_ref,
+    sem,
+    coarse_ref,
     over_in_ref,
-    packed_a_ref,
-    packed_i_ref,
-    tiles_ref,
-    total_ref,
-    projected_ref,
-    over_out_ref,
-    fields_ref,
-    sems,
+    field_ref,
+    ring_sems,
 ):
     step = pl.program_id(0)
-    side = total_ref.shape[1]
-    depth = coarse_a_ref.shape[1]
-    cols = packed_i_ref.shape[0]
-    copies = (
-        pltpu.make_async_copy(
-            packed_a_ref.at[:, pl.ds(depth, blocks_dev * side), :], over_out_ref, sems.at[0]
-        ),
-        pltpu.make_async_copy(
-            packed_i_ref.at[:, pl.ds(blocks_dev * depth, blocks_dev * side), :],
-            fields_ref.at[pl.ds(0, cols)],
-            sems.at[1],
-        ),
+    side = out_ref.shape[1]
+    depth = packed_b_ref.shape[1]
+
+    def reads(block, place):
+        slot = slots_ref[block]
+        owner, local = block // blocks_dev, block % blocks_dev
+        over_rows = pl.ds(pl.multiple_of(local * depth, depth), depth)
+        field_rows = pl.ds(pl.multiple_of(blocks_dev * depth + local * side, side), side)
+        sources = (
+            (packed_a_ref.at[slot, pl.ds(0, depth), :], coarse_ref.at[place, 0]),
+            (packed_b_ref.at[slot], coarse_ref.at[place, 1]),
+            (packed_i_ref.at[owner, over_rows, :], over_in_ref.at[place]),
+            (packed_i_ref.at[owner, field_rows, :], field_ref.at[place]),
+        )
+        return [
+            pltpu.make_async_copy(src, dst, ring_sems.at[place, n])
+            for n, (src, dst) in enumerate(sources)
+        ]
+
+    copy = pltpu.make_async_copy(
+        packed_a_ref.at[:, pl.ds(depth, blocks_dev * side), :], over_out_ref, sem
     )
 
     @pl.when(step == 0)
     def _():
-        for copy in copies:
-            copy.start()
-        total_ref[...] = jnp.zeros_like(total_ref)
-        fields_ref[cols] = jnp.zeros(fields_ref.shape[1:], fields_ref.dtype)
-
-    @pl.when(step < spread)
+        for block in range(ring):
+            for read in reads(block, block):
+                read.start()
+        copy.start()
+        products_ref[2 * spread] = jnp.zeros(products_ref.shape[1:], products_ref.dtype)
+
+    place = step % ring
+    for read in reads(step, place):
+        read.wait()
+    for a in range(2):
+        projected = jnp.dot(
+            coarse_ref[place, a], over_in_ref[place], preferred_element_type=jnp.float32
+        ).astype(jnp.bfloat16)
+        projected_ref[a] = projected
+        products_ref[step * 2 + a] = jnp.dot(
+            projected, field_ref[place], preferred_element_type=jnp.float32
+        )
+
+    @pl.when(step + ring < spread)
     def _():
-        for a, ref in enumerate((coarse_a_ref, coarse_b_ref)):
-            projected_ref[step * 2 + a] = jnp.dot(
-                ref[0], over_in_ref[0], preferred_element_type=jnp.float32
-            ).astype(jnp.bfloat16)
-
-    @pl.when(step == spread)
+        for read in reads(step + ring, place):
+            read.start()
+
+    @pl.when(step == pl.num_programs(0) - 1)
     def _():
-        for copy in copies:
-            copy.wait()
-
-    start = (step - spread) * chunk_pairs
-
-    @pl.when((step >= spread) & (start < used_ref[0]))
-    def _():
-        def group(g, carry):
-            adds = []
-            for k in range(unroll_pairs):
-                local = g * unroll_pairs + k
-                pair = start + local
-                block, first, second = out_ref_idx[pair], first_idx[pair], second_idx[pair]
-                a = point_idx[pair]
-                left = jnp.minimum(first, spread - 1) * 2 + a
-                right = jnp.minimum(second, spread - 1) * 2 + a
-                both = jnp.concatenate([projected_ref[left], projected_ref[right]], axis=1)
-                tile = jnp.dot(
-                    block_of(over_out_ref, block, blocks_dev, side),
-                    both,
-                    preferred_element_type=jnp.float32,
-                ).astype(jnp.bfloat16)
-                tiles_ref[local] = tile
-                adds.append(add_pair(total_ref, fields_ref, tile, block, first, second))
-            for ref, block, product in adds:
-                ref[block] += product
-            return carry
-
-        lax.fori_loop(0, chunk_pairs // unroll_pairs, group, 0)
+        copy.wait()
+        sum_products(
+            members_ref, base_ref, pairs_ref, products_ref, sums_ref, over_out_ref, out_ref
+        )
 
 
 def apply_kernel_body(
-    out_ref_idx,
-    first_idx,
-    second_idx,
-    used_ref,
-    tiles_ref,
+    blocks_dev,
+    spread,
+    members_ref,
+    base_ref,
+    pairs_ref,
+    projected_ref,
     pieces_ref,
-    total_ref,
-    fields_ref,
+    packed_a_ref,
+    out_ref,
+    products_ref,
+    sums_ref,
+    over_out_ref,
+    sem,
+    held_ref,
+    group_sems,
 ):
     step = pl.program_id(0)
-    cols = pieces_ref.shape[0]
+    side = out_ref.shape[1]
+    depth = projected_ref.shape[1]
+    groups = spread // apply_group
+    reads = [
+        pltpu.make_async_copy(
+            projected_ref.at[pl.ds(2 * apply_group * g, 2 * apply_group)],
+            held_ref.at[pl.ds(2 * apply_group * g, 2 * apply_group)],
+            group_sems.at[g],
+        )
+        for g in range(groups)
+    ]
+    copy = pltpu.make_async_copy(
+        packed_a_ref.at[:, pl.ds(depth, blocks_dev * side), :], over_out_ref, sem
+    )
 
     @pl.when(step == 0)
     def _():
-        total_ref[...] = jnp.zeros_like(total_ref)
-        fields_ref[pl.ds(0, cols)] = pieces_ref[...]
-        fields_ref[cols] = jnp.zeros(fields_ref.shape[1:], fields_ref.dtype)
-
-    start = step * chunk_pairs
-
-    @pl.when(start < used_ref[0])
+        for read in reads:
+            read.start()
+        copy.start()
+        products_ref[2 * spread] = jnp.zeros(products_ref.shape[1:], products_ref.dtype)
+
+    for g, read in enumerate(reads):
+        pl.when(step == g)(read.wait)
+
+    for g in range(apply_group):
+        block = step * apply_group + g
+        field = block_of(pieces_ref, block, blocks_dev, side)
+        for a in range(2):
+            products_ref[block * 2 + a] = jnp.dot(
+                held_ref[block * 2 + a], field, preferred_element_type=jnp.float32
+            )
+
+    @pl.when(step == pl.num_programs(0) - 1)
     def _():
-        def group(g, carry):
-            adds = []
-            for k in range(chunk_pairs):
-                local = g * chunk_pairs + k
-                pair = start + local
-                adds.append(
-                    add_pair(
-                        total_ref,
-                        fields_ref,
-                        tiles_ref[local],
-                        out_ref_idx[pair],
-                        first_idx[pair],
-                        second_idx[pair],
-                    )
-                )
-            for ref, block, product in adds:
-                ref[block] += product
-            return carry
-
-        lax.fori_loop(0, chunk_pairs // chunk_pairs, group, 0)
+        copy.wait()
+        sum_products(
+            members_ref, base_ref, pairs_ref, products_ref, sums_ref, over_out_ref, out_ref
+        )
 
 
 def gather_kernel(a_ref, b_ref, i_ref, out_a, out_b, out_i, send_sem, recv_sem, own_sem):
@@ -452,88 +481,76 @@
     )(partial, linear)
 
 
-def build_tiles(in_slots, tables, packed_a, packed_b, packed_i, pairs_max, blocks_dev, side):
+def apply_scratch(rows, blocks_dev, spread, depth, side, width):
+    return [
+        pltpu.VMEM((2 * spread + 1, depth, width), jnp.float32),
+        pltpu.VMEM((rows * blocks_dev, depth, width), jnp.bfloat16),
+        pltpu.VMEM((rows, blocks_dev * side, depth), jnp.bfloat16),
+        pltpu.SemaphoreType.DMA,
+    ]
+
+
+def project_and_apply(in_slots, tables, packed_a, packed_b, packed_i, blocks_dev, side):
     rows, cols = packed_a.shape[0], packed_i.shape[0]
     depth = packed_b.shape[1]
     width = packed_i.shape[2]
     spread, depth_out = cols * blocks_dev, rows * blocks_dev
-    chunks = pairs_max // chunk_pairs
-
-    def tile_chunk(s, *refs):
-        last = jnp.maximum((refs[5][0] + chunk_pairs - 1) // chunk_pairs - 1, 0)
-        return (jnp.clip(s - spread, 0, last), 0, 0)
-
-    def coarse_at(s, slots, *refs):
-        return (slots[jnp.minimum(s, spread - 1)], 0, 0)
-
-    def over_in_at(s, *refs):
-        block = jnp.minimum(s, spread - 1)
-        return (block // blocks_dev, block % blocks_dev, 0)
-
+    anywhere = pl.BlockSpec(memory_space=pl.ANY)
     grid_spec = pltpu.PrefetchScalarGridSpec(
-        num_scalar_prefetch=6,
-        grid=(spread + chunks,),
-        in_specs=[
-            pl.BlockSpec((1, depth, depth), coarse_at),
-            pl.BlockSpec((1, depth, depth), coarse_at),
-            pl.BlockSpec((1, depth, side), over_in_at),
-            pl.BlockSpec(memory_space=pl.ANY),
-            pl.BlockSpec(memory_space=pl.ANY),
-        ],
+        num_scalar_prefetch=4,
+        grid=(spread,),
+        in_specs=[anywhere] * 3,
         out_specs=[
-            pl.BlockSpec((chunk_pairs, side, 2 * side), tile_chunk),
+            pl.BlockSpec((2, depth, side), lambda s, *refs: (s, 0, 0)),
             pl.BlockSpec((depth_out, side, width), lambda s, *refs: (0, 0, 0)),
         ],
         scratch_shapes=[
-            pltpu.VMEM((spread * 2, depth, side), jnp.bfloat16),
-            pltpu.VMEM((rows, blocks_dev * side, depth), jnp.bfloat16),
-            pltpu.VMEM((cols + 1, blocks_dev * side, width), jnp.bfloat16),
-            pltpu.SemaphoreType.DMA((2,)),
+            *apply_scratch(rows, blocks_dev, spread, depth, side, width),
+            pltpu.VMEM((ring, 2, depth, depth), jnp.bfloat16),
+            pltpu.VMEM((ring, depth, side), jnp.bfloat16),
+            pltpu.VMEM((ring, side, width), jnp.bfloat16),
+            pltpu.SemaphoreType.DMA((ring, 4)),
         ],
     )
     return pl.pallas_call(
         functools.partial(build_kernel, blocks_dev, spread),
         grid_spec=grid_spec,
         out_shape=[
-            jax.ShapeDtypeStruct((pairs_max, side, 2 * side), jnp.bfloat16),
+            jax.ShapeDtypeStruct((2 * spread, depth, side), jnp.bfloat16),
             jax.ShapeDtypeStruct((depth_out, side, width), jnp.float32),
         ],
         compiler_params=pltpu.CompilerParams(vmem_limit_bytes=60 * 1024 * 1024),
-        name="build_tiles",
-    )(in_slots, *tables, packed_a, packed_b, packed_i, packed_a, packed_i)
-
-
-def apply_tiles(tables, tiles, pieces, depth_out):
-    pairs_max, side, _ = tiles.shape
-    cols, rows_dev, width = pieces.shape
-    out_idx, first, second, _, used = tables
-
-    def tile_chunk(s, *refs):
-        last = jnp.maximum((refs[3][0] + chunk_pairs - 1) // chunk_pairs - 1, 0)
-        return (jnp.minimum(s, last), 0, 0)
-
-    def held(s, *refs):
-        return (0, 0, 0)
-
+        name="project_and_apply",
+    )(in_slots, *tables, packed_a, packed_b, packed_i)
+
+
+def apply_again(tables, projected, pieces, packed_a, blocks_dev):
+    rows = packed_a.shape[0]
+    _, depth, side = projected.shape
+    cols, _, width = pieces.shape
+    spread, depth_out = cols * blocks_dev, rows * blocks_dev
     grid_spec = pltpu.PrefetchScalarGridSpec(
-        num_scalar_prefetch=4,
-        grid=(pairs_max // chunk_pairs,),
+        num_scalar_prefetch=3,
+        grid=(spread // apply_group,),
         in_specs=[
-            pl.BlockSpec((chunk_pairs, side, 2 * side), tile_chunk),
-            pl.BlockSpec(pieces.shape, held),
+            pl.BlockSpec(memory_space=pl.ANY),
+            pl.BlockSpec(pieces.shape, lambda s, *refs: (0, 0, 0)),
+            pl.BlockSpec(memory_space=pl.ANY),
         ],
-        out_specs=pl.BlockSpec((depth_out, side, width), held),
+        out_specs=pl.BlockSpec((depth_out, side, width), lambda s, *refs: (0, 0, 0)),
         scratch_shapes=[
-            pltpu.VMEM((cols + 1, rows_dev, width), jnp.bfloat16),
+            *apply_scratch(rows, blocks_dev, spread, depth, side, width),
+            pltpu.VMEM(projected.shape, jnp.bfloat16),
+            pltpu.SemaphoreType.DMA((spread // apply_group,)),
         ],
     )
     return pl.pallas_call(
-        apply_kernel_body,
+        functools.partial(apply_kernel_body, blocks_dev, spread),
         grid_spec=grid_spec,
         out_shape=jax.ShapeDtypeStruct((depth_out, side, width), jnp.float32),
         compiler_params=pltpu.CompilerParams(vmem_limit_bytes=60 * 1024 * 1024),
-        name="apply_tiles",
-    )(out_idx, first, second, used, tiles, pieces)
+        name="apply_again",
+    )(*tables, projected, pieces, packed_a)
 
 
 def on_device(
@@ -549,7 +566,6 @@
     spread = cols_count * blocks_dev
     depth_out = rows_count * blocks_dev
     pairs_max = (tile_codes.shape[1] + depth_out) // 2
-    pairs_max = -(-pairs_max // chunk_pairs) * chunk_pairs
     index_out = jnp.arange(depth_out, dtype=jnp.int32)
     index_in = jnp.arange(spread, dtype=jnp.int32)
     out_blocks = (
@@ -578,11 +594,11 @@
     def by_row(partial):
         return partial.reshape(rows_count, -1, width_vec)
 
-    tiles, partial = build_tiles(
-        in_slots, tables, packed_a, packed_b, packed_i, pairs_max, blocks_dev, tile_side
+    projected, partial = project_and_apply(
+        in_slots, tables, packed_a, packed_b, packed_i, blocks_dev, tile_side
     )
     first_step, pieces = exchange(by_row(partial), linear(vectors), True)
-    partial = apply_tiles(tables, tiles, pieces, depth_out)
+    partial = apply_again(tables, projected, pieces, packed_a, blocks_dev)
     kernel_part = exchange(by_row(partial), vectors, False)
     second_step = 2.0 * ((linear(first_step) + kernel_part) / spectrum_half) - vectors
     return first_step, second_step

time: 246 us -> 218 us (0.89)
  Pallas kernels: 227 us -> 200 us
    pallas_call x2, Pallas kernels: 83.9 us -> 58.9 us  [exchange(): pl.pallas_call(functools.partial(exchange_kernel, spread_on), in_specs=[v...]
where the time goes in v4:
time: 218 us; the launch traced here: 217 us
  Pallas kernels  200 us (92%)
  other arithmetic  11.8 us (5%)
  local copies, waits for them, and re-layouts  3.12 us (1%)
    pallas_call x1, Pallas kernels, gather_all(): pl.pallas_call(gather_kernel, in_specs=[vmem, vmem, vmem], out_specs=[any...  91 us
    pallas_call x2, Pallas kernels, exchange(): pl.pallas_call(functools.partial(exchange_kernel, spread_on), in_specs=[v...  58.9 us
    pallas_call x1, Pallas kernels, project_and_apply(): pl.pallas_call(functools.partial(build_kernel, blocks_dev, spread), grid_...  34.4 us
    pallas_call x1, Pallas kernels, apply_again(): pl.pallas_call(functools.partial(apply_kernel_body, blocks_dev, spread),...  16 us

profile of v4, /device:TPU:1, one launch (start us, length us, event | category | flops | bytes accessed | tf_op | source)
XLA Modules:
  0.0 216.9 jit_solution(11311958165768677125)
XLA Ops:
  0.6 0.0 copy-start.1
  1.4 0.9 select_reduce_fusion.3
  2.3 0.9 select_reduce_fusion.2
  3.2 1.3 select_reduce_fusion.5.slots_ref
  4.5 1.0 fusion.1
  5.5 0.1 reshape.159
  5.6 0.1 reduce_sum.65
  5.7 0.1 copy.12
  5.8 0.2 select_reduce_fusion.1
  6.0 0.0 copy-start.4
  6.0 0.1 select_reduce_fusion.4.base_ref
  6.1 0.0 copy-start.5
  6.2 0.1 copy.13
  6.2 0.1 add.139
  6.3 0.1 add_add_fusion
  6.4 0.1 add.149
  6.5 0.3 select_reduce_fusion
  6.8 0.6 add_select_fusion.members_ref
  7.4 1.8 multiply_subtract_fusion.1
  9.2 1.2 copy.14
  10.4 1.8 pad_maximum_fusion.1.i_ref
  12.2 0.0 copy-done.1
  12.2 0.9 slice_bitcast_fusion
  13.1 0.0 copy-done.4
  13.1 0.0 copy-done.5
  13.1 1.0 pad_maximum_fusion.a_ref
  14.1 91.0 %gather_all.1 = (bf16[16,896,512]{2,1,0:T(8,128)(2,1)}, bf16[16,512,512]{2,1,0:T(8,128)(2,1)}, bf16[8,1920,128]{2,1,0:T(8,128)(2,1)}) custom-call(bf16[896,512]{1,0:T(8,128)(2,1)} %pad_maximum_fusion.a_ref, bf16[512,512]{1,0:T(8,128)(2,1)} %get-tuple-element.16.b_ref, bf16[1920,128]{1,0:T(8,128)(2,1)} %pad_maximum_fusion.1.i_ref), custom_call_target="tpu_custom_call" | custom-call | tf_op jit(solution)/shard_map/gather_all/pallas_call | solution.py:349
  105.1 34.4 %project_and_apply.1 = (bf16[48,512,128]{2,1,0:T(8,128)(2,1)}, f32[48,128,128]{2,1,0:T(8,128)}) custom-call(s32[24]{0:T(128)} %select_reduce_fusion.5.slots_ref, s32[480]{0:T(512)} %add_select_fusion.members_ref, s32[48]{0:T(128)} %copy-done.5, s32[48]{0:T(128)} %copy-done.4, bf16[16,896,512]{2,1,0:T(8,128)(2,1)} %get-tuple-element.9.packed_a_ref, ...), custom_call_target="tpu_custom_call" | custom-call | tf_op jit(solution)/shard_map/project_and_apply/pallas_call | solution.py:515
  139.5 34.7 %exchange_spread.1 = (f32[384,128]{1,0:T(8,128)}, bf16[8,384,128]{2,1,0:T(8,128)(2,1)}) custom-call(f32[16,384,128]{2,1,0:T(8,128)} %bitcast.13, f32[384,128]{1,0:T(8,128)} %get-tuple-element.18.linear_ref), custom_call_target="tpu_custom_call" | custom-call | tf_op jit(solution)/shard_map/exchange_spread/pallas_call | solution.py:471
  174.2 16.0 %apply_again.1 = f32[48,128,128]{2,1,0:T(8,128)} custom-call(s32[480]{0:T(512)} %add_select_fusion.members_ref, s32[48]{0:T(128)} %copy-done.5, s32[48]{0:T(128)} %copy-done.4, bf16[48,512,128]{2,1,0:T(8,128)(2,1)} %get-tuple-element.14.projected_ref, bf16[8,384,128]{2,1,0:T(8,128)(2,1)} %get-tuple-element.15.pieces_ref, ...), custom_call_target="tpu_custom_call" | custom-call | tf_op jit(solution)/shard_map/apply_again/pallas_call | solution.py:547
  190.2 0.0 copy-start
  190.2 0.0 copy-start.2
  190.2 0.0 copy-start.3
  190.2 24.2 %exchange.1 = f32[384,128]{1,0:T(8,128)} custom-call(f32[16,384,128]{2,1,0:T(8,128)} %bitcast.12, f32[384,128]{1,0:T(8,128)} %linear_ref.1), custom_call_target="tpu_custom_call" | custom-call | tf_op jit(solution)/shard_map/exchange/pallas_call | solution.py:471
  214.4 0.0 copy-done
  214.4 0.0 copy-done.2
  214.4 0.0 copy-done.3
  214.4 1.7 multiply_subtract_fusion
  216.2 0.7 copy.17
  (11 shorter events, 0.1 us)
Async XLA Ops:
  0.6 11.6 %copy-start.1 = (bf16[2,1,512,512]{3,2,1,0:T(8,128)(2,1)S(1)}, bf16[2,1,512,512]{3,2,1,0:T(8,128)(2,1)}, u32[]{:S(2)}) copy-start(bf16[2,1,512,512]{3,2,1,0:T(8,128)(2,1)} %param.11) | copy-start | bytes 3145732
  6.0 7.1 %copy-start.4 = (s32[48]{0:T(128)}, s32[48]{0:T(128)S(1)}, u32[]{:S(2)}) copy-start(s32[48]{0:T(128)S(1)} %and_select_fusion.2.pairs_ref) | copy-start | bytes 580
  6.1 6.9 %copy-start.5 = (s32[48]{0:T(128)}, s32[48]{0:T(128)S(1)}, u32[]{:S(2)}) copy-start(s32[48]{0:T(128)S(1)} %select_reduce_fusion.4.base_ref) | copy-start | bytes 580
  190.2 24.2 %copy-start = (f32[384,128]{1,0:T(8,128)S(1)}, f32[384,128]{1,0:T(8,128)}, u32[]{:S(2)}) copy-start(f32[384,128]{1,0:T(8,128)} %linear_ref.1) | copy-start | bytes 589828
  190.2 24.2 %copy-start.2 = (f32[384,128]{1,0:T(8,128)S(1)}, f32[384,128]{1,0:T(8,128)}, u32[]{:S(2)}) copy-start(f32[384,128]{1,0:T(8,128)} %get-tuple-element.22) | copy-start | bytes 589828
  190.2 24.2 %copy-start.3 = (f32[384]{0:T(512)S(1)}, f32[384]{0:T(512)}, u32[]{:S(2)}) copy-start(f32[384]{0:T(512)} %param.9) | copy-start | bytes 4612

commit v5 on v4

--- a/solution.py
+++ b/solution.py
@@ -11,6 +11,8 @@
 spectrum_half = 3.0
 unroll_blocks = 4
 apply_group = 4
+list_group = 4
+sum_rows = 128
 ring = 6
 gather_copies = 53
 block_parts = 3
@@ -22,24 +24,24 @@
     return jnp.sum(jnp.where(matches, values_table[None, :], 0), axis=1)
 
 
-def pair_tables(codes, count, depth_out, spread, points, pairs_max):
+def list_tables(codes, count, depth_out, spread, points, groups_max):
     slots = jnp.arange(codes.shape[0], dtype=jnp.int32)
     all_codes = jnp.arange(depth_out * spread, dtype=jnp.int32)
     hits = (codes[:, None] == all_codes[None, :]) & (slots < count)[:, None]
     mask = jnp.any(hits, axis=0).astype(jnp.int32).reshape(depth_out, spread)
     filled = jnp.sum(mask, axis=1)
-    pairs = (filled + 1) // 2
+    groups = (filled + list_group - 1) // list_group
     index_out = jnp.arange(depth_out, dtype=jnp.int32)
     index_in = jnp.arange(spread, dtype=jnp.int32)
-    base = jnp.sum(jnp.where(index_out[None, :] < index_out[:, None], pairs[None, :], 0), axis=1)
+    base = jnp.sum(jnp.where(index_out[None, :] < index_out[:, None], groups[None, :], 0), axis=1)
     rank = jnp.sum(
         jnp.where(index_in[None, None, :] < index_in[None, :, None], mask[:, None, :], 0), axis=2
     )
-    place = jnp.where(mask > 0, 2 * base[:, None] + rank, -1).reshape(-1)
+    place = jnp.where(mask > 0, list_group * base[:, None] + rank, -1).reshape(-1)
     product = (index_in[None, :] * 2 + points[:, None]).reshape(-1)
-    spots = jnp.arange(2 * pairs_max, dtype=jnp.int32)
+    spots = jnp.arange(list_group * groups_max, dtype=jnp.int32)
     found = jnp.sum(jnp.where(spots[:, None] == place[None, :], product[None, :] + 1, 0), axis=1)
-    return jnp.where(found > 0, found - 1, 2 * spread), base, pairs
+    return jnp.where(found > 0, found - 1, 2 * spread), base, groups
 
 
 def block_of(ref, block, blocks_dev, side):
@@ -47,23 +49,27 @@
     return ref[block // blocks_dev, rows, :]
 
 
-def sum_products(members_ref, base_ref, pairs_ref, products_ref, sums_ref, over_out_ref, out_ref):
+def sum_products(members_ref, base_ref, groups_ref, products_ref, sums_ref, over_out_ref, out_ref):
     depth_out, side, width = out_ref.shape
     blocks_dev = over_out_ref.shape[1] // side
     depth = products_ref.shape[1]
-    half = depth // 2
 
     def add_up(q, carry):
         start = base_ref[q]
-        stop = start + pairs_ref[q]
-        for c in range(2):
-            rows = pl.ds(c * half, half)
-
-            def add(pair, total):
-                first, second = members_ref[2 * pair], members_ref[2 * pair + 1]
-                return total + (products_ref[first, rows, :] + products_ref[second, rows, :])
-
-            total = lax.fori_loop(start, stop, add, jnp.zeros((half, width), jnp.float32))
+        stop = start + groups_ref[q]
+        for c in range(depth // sum_rows):
+            rows = pl.ds(c * sum_rows, sum_rows)
+
+            def add(group, total):
+                parts = [
+                    products_ref[members_ref[list_group * group + n], rows, :]
+                    for n in range(list_group)
+                ]
+                while len(parts) > 1:
+                    parts = [left + right for left, right in zip(parts[::2], parts[1::2])]
+                return total + parts[0]
+
+            total = lax.fori_loop(start, stop, add, jnp.zeros((sum_rows, width), jnp.float32))
             sums_ref[q, rows, :] = total.astype(sums_ref.dtype)
         return carry
 
@@ -88,7 +94,7 @@
     slots_ref,
     members_ref,
     base_ref,
-    pairs_ref,
+    groups_ref,
     packed_a_ref,
     packed_b_ref,
     packed_i_ref,
@@ -156,7 +162,7 @@
     def _():
         copy.wait()
         sum_products(
-            members_ref, base_ref, pairs_ref, products_ref, sums_ref, over_out_ref, out_ref
+            members_ref, base_ref, groups_ref, products_ref, sums_ref, over_out_ref, out_ref
         )
 
 
@@ -165,7 +171,7 @@
     spread,
     members_ref,
     base_ref,
-    pairs_ref,
+    groups_ref,
     projected_ref,
     pieces_ref,
     packed_a_ref,
@@ -215,7 +221,7 @@
     def _():
         copy.wait()
         sum_products(
-            members_ref, base_ref, pairs_ref, products_ref, sums_ref, over_out_ref, out_ref
+            members_ref, base_ref, groups_ref, products_ref, sums_ref, over_out_ref, out_ref
         )
 
 
@@ -475,7 +481,9 @@
         out_shape=out_shape,
         scratch_shapes=scratch + sems,
         compiler_params=pltpu.CompilerParams(
-            collective_id=1 if spread_on else 2, has_side_effects=True
+            collective_id=1 if spread_on else 2,
+            has_side_effects=True,
+            vmem_limit_bytes=16 * 1024 * 1024,
         ),
         name="exchange_spread" if spread_on else "exchange",
     )(partial, linear)
@@ -495,7 +503,7 @@
     depth = packed_b.shape[1]
     width = packed_i.shape[2]
     spread, depth_out = cols * blocks_dev, rows * blocks_dev
-    anywhere = pl.BlockSpec(memory_space=pl.ANY)
+    anywhere = pl.BlockSpec(memory_space=pltpu.HBM)
     grid_spec = pltpu.PrefetchScalarGridSpec(
         num_scalar_prefetch=4,
         grid=(spread,),
@@ -519,7 +527,7 @@
             jax.ShapeDtypeStruct((2 * spread, depth, side), jnp.bfloat16),
             jax.ShapeDtypeStruct((depth_out, side, width), jnp.float32),
         ],
-        compiler_params=pltpu.CompilerParams(vmem_limit_bytes=60 * 1024 * 1024),
+        compiler_params=pltpu.CompilerParams(vmem_limit_bytes=49 * 1024 * 1024),
         name="project_and_apply",
     )(in_slots, *tables, packed_a, packed_b, packed_i)
 
@@ -533,9 +541,9 @@
         num_scalar_prefetch=3,
         grid=(spread // apply_group,),
         in_specs=[
-            pl.BlockSpec(memory_space=pl.ANY),
+            pl.BlockSpec(memory_space=pltpu.HBM),
             pl.BlockSpec(pieces.shape, lambda s, *refs: (0, 0, 0)),
-            pl.BlockSpec(memory_space=pl.ANY),
+            pl.BlockSpec(memory_space=pltpu.HBM),
         ],
         out_specs=pl.BlockSpec((depth_out, side, width), lambda s, *refs: (0, 0, 0)),
         scratch_shapes=[
@@ -548,7 +556,7 @@
         functools.partial(apply_kernel_body, blocks_dev, spread),
         grid_spec=grid_spec,
         out_shape=jax.ShapeDtypeStruct((depth_out, side, width), jnp.float32),
-        compiler_params=pltpu.CompilerParams(vmem_limit_bytes=60 * 1024 * 1024),
+        compiler_params=pltpu.CompilerParams(vmem_limit_bytes=49 * 1024 * 1024),
         name="apply_again",
     )(*tables, projected, pieces, packed_a)
 
@@ -565,7 +573,7 @@
     points_col = coarse.shape[0]
     spread = cols_count * blocks_dev
     depth_out = rows_count * blocks_dev
-    pairs_max = (tile_codes.shape[1] + depth_out) // 2
+    groups_max = (tile_codes.shape[1] + (list_group - 1) * depth_out) // list_group
     index_out = jnp.arange(depth_out, dtype=jnp.int32)
     index_in = jnp.arange(spread, dtype=jnp.int32)
     out_blocks = (
@@ -574,8 +582,8 @@
     in_blocks = (row_id * cols_count + index_in // blocks_dev) * blocks_dev + index_in % blocks_dev
     in_slots = lookup(coarse_slot, lookup(fine_coarse, in_blocks))
     out_points = lookup(fine_coarse, out_blocks) - col_id * points_col
-    tables = pair_tables(
-        tile_codes[0], tile_count[0], depth_out, spread, out_points, pairs_max
+    tables = list_tables(
+        tile_codes[0], tile_count[0], depth_out, spread, out_points, groups_max
     )
 
     pair_energy = energies.reshape(-1, 1)

time: 218 us -> 206 us (0.945)
  Pallas kernels: 200 us -> 192 us
  other arithmetic: 11.8 us -> 9.15 us
    pallas_call x2, Pallas kernels: 58.9 us -> 47.5 us  [exchange(): pl.pallas_call(functools.partial(exchange_kernel, spread_on), in_specs=[v...]
    pallas_call x1, Pallas kernels: 34.4 us -> 37 us  [project_and_apply(): pl.pallas_call(functools.partial(build_kernel, blocks_dev, spread), grid_...]
where the time goes in v5:
time: 206 us
  Pallas kernels  192 us (93%)
  other arithmetic  9.15 us (4%)
  local copies, waits for them, and re-layouts  3.12 us (2%)
    pallas_call x1, Pallas kernels, gather_all(): pl.pallas_call(gather_kernel, in_specs=[vmem, vmem, vmem], out_specs=[any...  91 us
    pallas_call x2, Pallas kernels, exchange(): pl.pallas_call(functools.partial(exchange_kernel, spread_on), in_specs=[v...  47.5 us
    pallas_call x1, Pallas kernels, project_and_apply(): pl.pallas_call(functools.partial(build_kernel, blocks_dev, spread), grid_...  37 us
    pallas_call x1, Pallas kernels, apply_again(): pl.pallas_call(functools.partial(apply_kernel_body, blocks_dev, spread),...  16.9 us

profile of v5, /device:TPU:1, one launch (start us, length us, event | category | flops | bytes accessed | tf_op | source)
XLA Modules:
  0.0 206.3 jit_solution(6774663153677511513)
XLA Ops:
  0.6 0.0 copy-start.1
  1.4 0.9 select_reduce_fusion.3
  2.3 0.9 select_reduce_fusion.2
  3.2 0.7 select_reduce_fusion.5.slots_ref
  3.9 1.0 fusion.1
  5.0 0.1 reshape.159
  5.1 0.1 reduce_sum.65
  5.2 0.1 copy.12
  5.2 0.2 select_reduce_fusion.1
  5.4 0.1 select_reduce_fusion.4.base_ref
  5.6 0.1 copy.13
  5.6 0.1 add.139
  5.7 0.1 add_add_fusion
  5.8 0.1 add.149
  5.9 0.4 select_reduce_fusion
  6.3 1.1 multiply_subtract_fusion.1
  7.4 1.2 copy.14
  8.6 1.8 pad_maximum_fusion.1.i_ref
  10.4 0.0 copy-done.1
  10.4 0.9 slice_bitcast_fusion
  11.3 1.0 pad_maximum_fusion.a_ref
  12.3 91.0 %gather_all.1 = (bf16[16,896,512]{2,1,0:T(8,128)(2,1)}, bf16[16,512,512]{2,1,0:T(8,128)(2,1)}, bf16[8,1920,128]{2,1,0:T(8,128)(2,1)}) custom-call(bf16[896,512]{1,0:T(8,128)(2,1)} %pad_maximum_fusion.a_ref, bf16[512,512]{1,0:T(8,128)(2,1)} %get-tuple-element.16.b_ref, bf16[1920,128]{1,0:T(8,128)(2,1)} %pad_maximum_fusion.1.i_ref), custom_call_target="tpu_custom_call" | custom-call | tf_op jit(solution)/shard_map/gather_all/pallas_call | solution.py:355
  103.3 37.0 %project_and_apply.1 = (bf16[48,512,128]{2,1,0:T(8,128)(2,1)}, f32[48,128,128]{2,1,0:T(8,128)S(1)}) custom-call(s32[24]{0:T(128)S(1)} %select_reduce_fusion.5.slots_ref, s32[576]{0:T(1024)S(1)} %add_select_fusion.members_ref, s32[48]{0:T(128)S(1)} %select_reduce_fusion.4.base_ref, s32[48]{0:T(128)S(1)} %and_select_fusion.2.groups_ref, ...), custom_call_target="tpu_custom_call" | custom-call | tf_op jit(solution)/shard_map/project_and_apply/pallas_call | solution.py:523
  140.3 28.6 %exchange_spread.1 = (f32[384,128]{1,0:T(8,128)S(1)}, bf16[8,384,128]{2,1,0:T(8,128)(2,1)S(1)}) custom-call(f32[16,384,128]{2,1,0:T(8,128)S(1)} %bitcast.13, f32[384,128]{1,0:T(8,128)S(1)} %get-tuple-element.18.linear_ref), custom_call_target="tpu_custom_call" | custom-call | tf_op jit(solution)/shard_map/exchange_spread/pallas_call | solution.py:477
  169.0 0.0 copy-start
  169.0 16.9 %apply_again.1 = f32[48,128,128]{2,1,0:T(8,128)S(1)} custom-call(s32[576]{0:T(1024)S(1)} %add_select_fusion.members_ref, s32[48]{0:T(128)S(1)} %select_reduce_fusion.4.base_ref, s32[48]{0:T(128)S(1)} %and_select_fusion.2.groups_ref, bf16[48,512,128]{2,1,0:T(8,128)(2,1)} %get-tuple-element.14.projected_ref, ...), custom_call_target="tpu_custom_call" | custom-call | tf_op jit(solution)/shard_map/apply_again/pallas_call | solution.py:555
  185.9 0.0 copy-start.2
  185.9 0.0 copy-done
  185.9 18.8 %exchange.1 = f32[384,128]{1,0:T(8,128)S(1)} custom-call(f32[16,384,128]{2,1,0:T(8,128)S(1)} %bitcast.12, f32[384,128]{1,0:T(8,128)S(1)} %copy-done), custom_call_target="tpu_custom_call" | custom-call | tf_op jit(solution)/shard_map/exchange/pallas_call | solution.py:477
  204.8 0.0 copy-done.2
  204.8 0.8 multiply_subtract_fusion
  205.6 0.7 copy.17
  (12 shorter events, 0.1 us)
Async XLA Ops:
  0.6 9.8 %copy-start.1 = (bf16[2,1,512,512]{3,2,1,0:T(8,128)(2,1)S(1)}, bf16[2,1,512,512]{3,2,1,0:T(8,128)(2,1)}, u32[]{:S(2)}) copy-start(bf16[2,1,512,512]{3,2,1,0:T(8,128)(2,1)} %param.11) | copy-start | bytes 3145732
  169.0 17.0 %copy-start = (f32[384,128]{1,0:T(8,128)S(1)}, f32[384,128]{1,0:T(8,128)}, u32[]{:S(2)}) copy-start(f32[384,128]{1,0:T(8,128)} %linear_ref.1) | copy-start | bytes 589828
  185.9 18.9 %copy-start.2 = (f32[384]{0:T(512)S(1)}, f32[384]{0:T(512)}, u32[]{:S(2)}) copy-start(f32[384]{0:T(512)} %param.9) | copy-start | bytes 4612

commit v6 on v5

--- a/solution.py
+++ b/solution.py
@@ -13,8 +13,8 @@
 apply_group = 4
 list_group = 4
 sum_rows = 128
-ring = 6
-gather_copies = 53
+ring_groups = 3
+gather_copies = 54
 block_parts = 3
 MESH = pl.DeviceIdType.MESH
 
@@ -135,28 +135,31 @@
 
     @pl.when(step == 0)
     def _():
-        for block in range(ring):
+        for block in range(ring_groups * blocks_dev):
             for read in reads(block, block):
                 read.start()
         copy.start()
         products_ref[2 * spread] = jnp.zeros(products_ref.shape[1:], products_ref.dtype)
 
-    place = step % ring
-    for read in reads(step, place):
-        read.wait()
-    for a in range(2):
-        projected = jnp.dot(
-            coarse_ref[place, a], over_in_ref[place], preferred_element_type=jnp.float32
-        ).astype(jnp.bfloat16)
-        projected_ref[a] = projected
-        products_ref[step * 2 + a] = jnp.dot(
-            projected, field_ref[place], preferred_element_type=jnp.float32
-        )
-
-    @pl.when(step + ring < spread)
+    first_place = step % ring_groups * blocks_dev
+    for local in range(blocks_dev):
+        block, place = step * blocks_dev + local, first_place + local
+        for read in reads(block, place):
+            read.wait()
+        for a in range(2):
+            projected = jnp.dot(
+                coarse_ref[place, a], over_in_ref[place], preferred_element_type=jnp.float32
+            ).astype(jnp.bfloat16)
+            projected_ref[2 * local + a] = projected
+            products_ref[block * 2 + a] = jnp.dot(
+                projected, field_ref[place], preferred_element_type=jnp.float32
+            )
+
+    @pl.when(step + ring_groups < pl.num_programs(0))
     def _():
-        for read in reads(step + ring, place):
-            read.start()
+        for local in range(blocks_dev):
+            for read in reads((step + ring_groups) * blocks_dev + local, first_place + local):
+                read.start()
 
     @pl.when(step == pl.num_programs(0) - 1)
     def _():
@@ -225,7 +228,7 @@
         )
 
 
-def gather_kernel(a_ref, b_ref, i_ref, out_a, out_b, out_i, send_sem, recv_sem, own_sem):
+def gather_kernel(coarse_ref, across_ref, i_ref, out_a, out_b, out_i, send_sem, recv_sem, own_sem):
     row, col = lax.axis_index("row"), lax.axis_index("col")
     h, z, k = row // 8, row // 2 % 4, row % 2
     l, x = col // 4, col % 4
@@ -249,7 +252,10 @@
         size = ref.shape[0] // 2
         return [pl.ds(s * size, size) for s in range(2)]
 
-    half_a, half_b, half_i = halves(a_ref), halves(b_ref), halves(i_ref)
+    depth = coarse_ref.shape[1]
+    a_own = (coarse_ref.at[0], across_ref)
+    half_a = [pl.ds(0, depth), pl.ds(depth, across_ref.shape[0])]
+    half_b, half_i = halves(coarse_ref.at[1]), halves(i_ref)
     copies, to_sibling = [], []
 
     def send(src, dst, device):
@@ -271,24 +277,28 @@
     def share(out, slot):
         to_sibling.append(send(out.at[slot], out.at[slot], sibling))
 
-    def forward(arrivals, out, slots, parts, devices):
+    def forward(arrivals, out, slots, parts, devices, flip=0):
         sent = []
         for d in range(2):
-            arrivals[d][d].wait_recv()
-            sent.append(pass_on(out, slots[d], parts[d], devices[d]))
-        arrivals[0][1].wait_recv()
-        arrivals[1][0].wait_recv()
+            arrivals[d][d ^ flip].wait_recv()
+            sent.append(pass_on(out, slots[d], parts[d ^ flip], devices[d]))
+        arrivals[0][1 ^ flip].wait_recv()
+        arrivals[1][flip].wait_recv()
         return sent
 
-    a_y = [send(a_ref.at[p], out_a.at[row, p], partner) for p in half_a]
-    b_z = [[send(b_ref.at[p], out_b.at[row, p], z_dev[d]) for p in half_b] for d in range(2)]
+    a_y = [send(src, out_a.at[row, p], partner) for src, p in zip(a_own, half_a)]
+    b_z = [
+        [send(coarse_ref.at[1, p], out_b.at[row, p], z_dev[d]) for p in half_b] for d in range(2)
+    ]
     i_x = [[send(i_ref.at[p], out_i.at[col, p], x_dev[d]) for p in half_i] for d in range(2)]
-    to_sibling.append(send(a_ref, out_a.at[row], sibling))
-    to_sibling.append(send(b_ref, out_b.at[row], sibling))
+    for src, p in zip(a_own, half_a):
+        to_sibling.append(send(src, out_a.at[row, p], sibling))
+    to_sibling.append(send(coarse_ref.at[1], out_b.at[row], sibling))
     own = [
-        pltpu.make_async_copy(a_ref, out_a.at[row], own_sem.at[0]),
-        pltpu.make_async_copy(b_ref, out_b.at[row], own_sem.at[1]),
-        pltpu.make_async_copy(i_ref, out_i.at[col], own_sem.at[2]),
+        pltpu.make_async_copy(a_own[0], out_a.at[row, half_a[0]], own_sem.at[0]),
+        pltpu.make_async_copy(a_own[1], out_a.at[row, half_a[1]], own_sem.at[1]),
+        pltpu.make_async_copy(coarse_ref.at[1], out_b.at[row], own_sem.at[2]),
+        pltpu.make_async_copy(i_ref, out_i.at[col], own_sem.at[3]),
     ]
     for copy in own:
         copy.start()
@@ -303,7 +313,9 @@
     other_cols = ((1 - l) * 4 + (x + 3) % 4, (1 - l) * 4 + (x + 1) % 4)
 
     b_zf = forward(b_z, out_b, z_rows, half_b, z_dev)
-    a_z = [[send(a_ref.at[p], out_a.at[row, p], z_dev[d]) for p in half_a] for d in range(2)]
+    a_z = [
+        [send(src, out_a.at[row, p], z_dev[d]) for src, p in zip(a_own, half_a)] for d in range(2)
+    ]
     for slot in z_rows:
         share(out_b, slot)
     a2_z = [[None, None], [None, None]]
@@ -313,7 +325,7 @@
             a2_z[d][s] = pass_on(out_a, other, half_a[s], z_dev[d])
     share(out_a, other)
     i_pair = send(i_ref, out_i.at[col], pair)
-    b_y = [send(b_ref, out_b.at[row], partner)]
+    b_y = [send(coarse_ref.at[1], out_b.at[row], partner)]
     for slot in z_rows:
         b_y.append(send(out_b.at[slot], out_b.at[slot], partner))
     i_xf = forward(i_x, out_i, x_cols, half_i, x_dev)
@@ -330,7 +342,7 @@
         a_zf[d].wait_recv()
     share(out_a, far)
     i2_xf = forward(i2_x, out_i, other_cols, half_i, x_dev)
-    a2_zf = forward(a2_z, out_a, other_rows, half_a, z_dev)
+    a2_zf = forward(a2_z, out_a, other_rows, half_a, z_dev, 1)
     for slot in other_rows:
         share(out_a, slot)
     for slot, copy in zip((other, *other_rows, other_far), b_y):
@@ -348,8 +360,9 @@
         copy.wait_send()
 
 
-def gather_all(a, b, i):
+def gather_all(coarse, across, i):
     rows, cols = lax.axis_size("row"), lax.axis_size("col")
+    depth = coarse.shape[1]
     vmem = pl.BlockSpec(memory_space=pltpu.VMEM)
     anywhere = pl.BlockSpec(memory_space=pl.ANY)
     return pl.pallas_call(
@@ -357,18 +370,18 @@
         in_specs=[vmem, vmem, vmem],
         out_specs=[anywhere] * 3,
         out_shape=[
-            jax.ShapeDtypeStruct((rows, *a.shape), a.dtype),
-            jax.ShapeDtypeStruct((rows, *b.shape), b.dtype),
+            jax.ShapeDtypeStruct((rows, depth + across.shape[0], depth), coarse.dtype),
+            jax.ShapeDtypeStruct((rows, depth, depth), coarse.dtype),
             jax.ShapeDtypeStruct((cols, *i.shape), i.dtype),
         ],
         scratch_shapes=[
             pltpu.SemaphoreType.DMA((gather_copies,)),
             pltpu.SemaphoreType.DMA((gather_copies,)),
-            pltpu.SemaphoreType.DMA((3,)),
+            pltpu.SemaphoreType.DMA((4,)),
         ],
         compiler_params=pltpu.CompilerParams(collective_id=0, has_side_effects=True),
         name="gather_all",
-    )(a, b, i)
+    )(coarse, across, i)
 
 
 def exchange_kernel(spread_on, partial_ref, linear_ref, *refs):
@@ -504,12 +517,13 @@
     width = packed_i.shape[2]
     spread, depth_out = cols * blocks_dev, rows * blocks_dev
     anywhere = pl.BlockSpec(memory_space=pltpu.HBM)
+    ring = ring_groups * blocks_dev
     grid_spec = pltpu.PrefetchScalarGridSpec(
         num_scalar_prefetch=4,
-        grid=(spread,),
+        grid=(cols,),
         in_specs=[anywhere] * 3,
         out_specs=[
-            pl.BlockSpec((2, depth, side), lambda s, *refs: (s, 0, 0)),
+            pl.BlockSpec((2 * blocks_dev, depth, side), lambda s, *refs: (s, 0, 0)),
             pl.BlockSpec((depth_out, side, width), lambda s, *refs: (0, 0, 0)),
         ],
         scratch_shapes=[
@@ -589,8 +603,8 @@
     pair_energy = energies.reshape(-1, 1)
     across = jnp.swapaxes(intersections, 1, 2).reshape(-1, pairs_coarse)
     packed_a, packed_b, packed_i = gather_all(
-        jnp.concatenate([coarse[0, 0], across], axis=0),
-        coarse[1, 0],
+        coarse[:, 0],
+        across,
         jnp.concatenate(
             [intersections.reshape(-1, tile_side), vectors.astype(jnp.bfloat16)], axis=0
         ),

time: 206 us -> 209 us (1.015)
  Pallas kernels: 192 us -> 197 us
    pallas_call x2, Pallas kernels: 47.5 us -> 53.9 us  [exchange(): pl.pallas_call(functools.partial(exchange_kernel, spread_on), in_specs=[v...]
where the time goes in v6:
time: 209 us; the launch traced here: 210 us
  Pallas kernels  197 us (94%)
  other arithmetic  8.17 us (4%)
  local copies, waits for them, and re-layouts  3 us (1%)
    pallas_call x1, Pallas kernels, gather_all(): pl.pallas_call(gather_kernel, in_specs=[vmem, vmem, vmem], out_specs=[any...  91.7 us
    pallas_call x2, Pallas kernels, exchange(): pl.pallas_call(functools.partial(exchange_kernel, spread_on), in_specs=[v...  53.9 us
    pallas_call x1, Pallas kernels, project_and_apply(): pl.pallas_call(functools.partial(build_kernel, blocks_dev, spread), grid_...  36 us
    pallas_call x1, Pallas kernels, apply_again(): pl.pallas_call(functools.partial(apply_kernel_body, blocks_dev, spread),...  15.6 us

profile of v6, /device:TPU:1, one launch (start us, length us, event | category | flops | bytes accessed | tf_op | source)
XLA Modules:
  0.0 209.8 jit_solution(2495782308835048127)
XLA Ops:
  1.3 0.9 select_reduce_fusion.3
  2.2 0.9 select_reduce_fusion.2
  3.1 0.7 select_reduce_fusion.5.slots_ref
  3.8 1.0 fusion.1
  4.9 0.1 reshape.159
  5.0 0.1 reduce_sum.65
  5.1 0.1 copy.12
  5.1 0.2 select_reduce_fusion.1
  5.3 0.1 select_reduce_fusion.4.base_ref
  5.5 0.1 copy.13
  5.5 0.1 add.139
  5.6 0.1 add_add_fusion
  5.7 0.1 add.149
  5.8 0.4 select_reduce_fusion
  6.2 1.1 multiply_subtract_fusion.1
  7.3 1.9 copy.14
  9.2 1.8 pad_maximum_fusion.i_ref
  11.1 91.7 %gather_all.1 = (bf16[16,896,512]{2,1,0:T(8,128)(2,1)}, bf16[16,512,512]{2,1,0:T(8,128)(2,1)}, bf16[8,1920,128]{2,1,0:T(8,128)(2,1)}) custom-call(bf16[2,512,512]{2,1,0:T(8,128)(2,1)} %bitcast.14, bf16[384,512]{1,0:T(8,128)(2,1)} %bitcast.13, bf16[1920,128]{1,0:T(8,128)(2,1)} %pad_maximum_fusion.i_ref), custom_call_target="tpu_custom_call" | custom-call | tf_op jit(solution)/shard_map/gather_all/pallas_call | solution.py:368
  102.8 36.0 %project_and_apply.1 = (bf16[48,512,128]{2,1,0:T(8,128)(2,1)}, f32[48,128,128]{2,1,0:T(8,128)S(1)}) custom-call(s32[24]{0:T(128)S(1)} %select_reduce_fusion.5.slots_ref, s32[576]{0:T(1024)S(1)} %add_select_fusion.members_ref, s32[48]{0:T(128)S(1)} %select_reduce_fusion.4.base_ref, s32[48]{0:T(128)S(1)} %and_select_fusion.2.groups_ref, ...), custom_call_target="tpu_custom_call" | custom-call | tf_op jit(solution)/shard_map/project_and_apply/pallas_call | solution.py:537
  138.8 30.5 %exchange_spread.1 = (f32[384,128]{1,0:T(8,128)S(1)}, bf16[8,384,128]{2,1,0:T(8,128)(2,1)S(1)}) custom-call(f32[16,384,128]{2,1,0:T(8,128)S(1)} %bitcast.10, f32[384,128]{1,0:T(8,128)S(1)} %get-tuple-element.16.linear_ref), custom_call_target="tpu_custom_call" | custom-call | tf_op jit(solution)/shard_map/exchange_spread/pallas_call | solution.py:490
  169.3 0.0 copy-start
  169.3 15.6 %apply_again.1 = f32[48,128,128]{2,1,0:T(8,128)S(1)} custom-call(s32[576]{0:T(1024)S(1)} %add_select_fusion.members_ref, s32[48]{0:T(128)S(1)} %select_reduce_fusion.4.base_ref, s32[48]{0:T(128)S(1)} %and_select_fusion.2.groups_ref, bf16[48,512,128]{2,1,0:T(8,128)(2,1)} %get-tuple-element.14.projected_ref, ...), custom_call_target="tpu_custom_call" | custom-call | tf_op jit(solution)/shard_map/apply_again/pallas_call | solution.py:569
  184.9 0.0 copy-start.1
  184.9 0.0 copy-done
  184.9 23.4 %exchange.1 = f32[384,128]{1,0:T(8,128)S(1)} custom-call(f32[16,384,128]{2,1,0:T(8,128)S(1)} %bitcast.9, f32[384,128]{1,0:T(8,128)S(1)} %copy-done), custom_call_target="tpu_custom_call" | custom-call | tf_op jit(solution)/shard_map/exchange/pallas_call | solution.py:490
  208.3 0.0 copy-done.1
  208.3 0.8 multiply_subtract_fusion
  209.1 0.7 copy.17
  (12 shorter events, 0.1 us)
Async XLA Ops:
  169.3 15.6 %copy-start = (f32[384,128]{1,0:T(8,128)S(1)}, f32[384,128]{1,0:T(8,128)}, u32[]{:S(2)}) copy-start(f32[384,128]{1,0:T(8,128)} %linear_ref.1) | copy-start | bytes 589828
  184.9 23.4 %copy-start.1 = (f32[384]{0:T(512)S(1)}, f32[384]{0:T(512)}, u32[]{:S(2)}) copy-start(f32[384]{0:T(512)} %param.9) | copy-start | bytes 4612

commit v7 on v6

--- a/solution.py
+++ b/solution.py
@@ -427,27 +427,32 @@
     side = partial_ref.shape[1] // block_parts
     parts = [pl.ds(t * side, side) for t in range(block_parts)]
     crossed = [
-        send(partial_ref.at[row_of(turn, 1 - k)], from_core.at[i], sibling)
-        for i, turn in enumerate(turns)
+        [
+            send(partial_ref.at[row_of(turn, 1 - k), p], from_core.at[i, p], sibling)
+            for i, turn in enumerate(turns)
+        ]
+        for p in parts
     ]
-    arrivals = []
-
-    def send_on(i):
+    arrivals, ready = [[] for _ in parts], []
+
+    def send_on(t, i):
         device = (row_of(turns[i], k), col)
-        arrivals.append([send(mine.at[i, p], landed.at[i, p], device) for p in parts])
-
-    for i in range(peers):
-        crossed[i].wait_recv()
-        mine[i] = (partial_ref[row_of(turns[i], k)] + from_core[i]).astype(mine.dtype)
-        if i > 0:
-            send_on(i - 1)
-    crossed[peers].wait_recv()
-    send_on(peers - 1)
+        arrivals[t].append(send(mine.at[i, parts[t]], landed.at[i, parts[t]], device))
+
+    for t, p in enumerate(parts):
+        for i in range(peers):
+            crossed[t][i].wait_recv()
+            mine[i, p] = (partial_ref[row_of(turns[i], k), p] + from_core[i, p]).astype(mine.dtype)
+            if ready:
+                send_on(*ready.pop())
+            ready.append((t, i))
+        crossed[t][peers].wait_recv()
+    send_on(*ready.pop())
     spreads, own = [], []
     for t, p in enumerate(parts):
         total = partial_ref[row, p] + from_core[peers, p]
         for i in range(peers - 1, -1, -1):
-            arrivals[i][t].wait_recv()
+            arrivals[t][i].wait_recv()
             total += landed[i, p].astype(jnp.float32)
         if spread_on:
             total = (linear_ref[p] + total) / spectrum_half
@@ -471,7 +476,7 @@
 def exchange(partial, linear, spread_on):
     rows, rows_dev, width = partial.shape
     cols = lax.axis_size("col")
-    count = 8 + 7 * block_parts * (2 if spread_on else 1)
+    count = block_parts * (8 + 7 * (2 if spread_on else 1))
     vmem = pl.BlockSpec(memory_space=pltpu.VMEM)
     block = jax.ShapeDtypeStruct((rows_dev, width), jnp.float32)
     scratch = [

time: 209 us -> 209 us (level)
  no operation moved by 1% of the time
where the time goes in v7:
time: 209 us; the launch traced here: 208 us
  Pallas kernels  196 us (94%)
  other arithmetic  8.17 us (4%)
  local copies, waits for them, and re-layouts  3 us (1%)
    pallas_call x1, Pallas kernels, gather_all(): pl.pallas_call(gather_kernel, in_specs=[vmem, vmem, vmem], out_specs=[any...  91.7 us
    pallas_call x2, Pallas kernels, exchange(): pl.pallas_call(functools.partial(exchange_kernel, spread_on), in_specs=[v...  55.9 us
    pallas_call x1, Pallas kernels, project_and_apply(): pl.pallas_call(functools.partial(build_kernel, blocks_dev, spread), grid_...  34.3 us
    pallas_call x1, Pallas kernels, apply_again(): pl.pallas_call(functools.partial(apply_kernel_body, blocks_dev, spread),...  13.7 us

profile of v7, /device:TPU:1, one launch (start us, length us, event | category | flops | bytes accessed | tf_op | source)
XLA Modules:
  0.0 208.2 jit_solution(15827185811637524611)
XLA Ops:
  1.3 0.9 select_reduce_fusion.3
  2.2 0.9 select_reduce_fusion.2
  3.1 0.7 select_reduce_fusion.5.slots_ref
  3.8 1.0 fusion.1
  4.9 0.1 reshape.159
  5.0 0.1 reduce_sum.65
  5.1 0.1 copy.12
  5.1 0.2 select_reduce_fusion.1
  5.3 0.1 select_reduce_fusion.4.base_ref
  5.5 0.1 copy.13
  5.5 0.1 add.139
  5.6 0.1 add_add_fusion
  5.7 0.1 add.149
  5.8 0.4 select_reduce_fusion
  6.2 1.1 multiply_subtract_fusion.1
  7.3 1.9 copy.14
  9.2 1.8 pad_maximum_fusion.i_ref
  11.1 91.7 %gather_all.1 = (bf16[16,896,512]{2,1,0:T(8,128)(2,1)}, bf16[16,512,512]{2,1,0:T(8,128)(2,1)}, bf16[8,1920,128]{2,1,0:T(8,128)(2,1)}) custom-call(bf16[2,512,512]{2,1,0:T(8,128)(2,1)} %bitcast.14, bf16[384,512]{1,0:T(8,128)(2,1)} %bitcast.13, bf16[1920,128]{1,0:T(8,128)(2,1)} %pad_maximum_fusion.i_ref), custom_call_target="tpu_custom_call" | custom-call | tf_op jit(solution)/shard_map/gather_all/pallas_call | solution.py:368
  102.8 34.3 %project_and_apply.1 = (bf16[48,512,128]{2,1,0:T(8,128)(2,1)}, f32[48,128,128]{2,1,0:T(8,128)S(1)}) custom-call(s32[24]{0:T(128)S(1)} %select_reduce_fusion.5.slots_ref, s32[576]{0:T(1024)S(1)} %add_select_fusion.members_ref, s32[48]{0:T(128)S(1)} %select_reduce_fusion.4.base_ref, s32[48]{0:T(128)S(1)} %and_select_fusion.2.groups_ref, ...), custom_call_target="tpu_custom_call" | custom-call | tf_op jit(solution)/shard_map/project_and_apply/pallas_call | solution.py:542
  137.1 36.3 %exchange_spread.1 = (f32[384,128]{1,0:T(8,128)S(1)}, bf16[8,384,128]{2,1,0:T(8,128)(2,1)S(1)}) custom-call(f32[16,384,128]{2,1,0:T(8,128)S(1)} %bitcast.10, f32[384,128]{1,0:T(8,128)S(1)} %get-tuple-element.16.linear_ref), custom_call_target="tpu_custom_call" | custom-call | tf_op jit(solution)/shard_map/exchange_spread/pallas_call | solution.py:495
  173.5 0.0 copy-start
  173.5 13.7 %apply_again.1 = f32[48,128,128]{2,1,0:T(8,128)S(1)} custom-call(s32[576]{0:T(1024)S(1)} %add_select_fusion.members_ref, s32[48]{0:T(128)S(1)} %select_reduce_fusion.4.base_ref, s32[48]{0:T(128)S(1)} %and_select_fusion.2.groups_ref, bf16[48,512,128]{2,1,0:T(8,128)(2,1)} %get-tuple-element.14.projected_ref, ...), custom_call_target="tpu_custom_call" | custom-call | tf_op jit(solution)/shard_map/apply_again/pallas_call | solution.py:574
  187.1 0.0 copy-start.1
  187.1 0.0 copy-done
  187.1 19.6 %exchange.1 = f32[384,128]{1,0:T(8,128)S(1)} custom-call(f32[16,384,128]{2,1,0:T(8,128)S(1)} %bitcast.9, f32[384,128]{1,0:T(8,128)S(1)} %copy-done), custom_call_target="tpu_custom_call" | custom-call | tf_op jit(solution)/shard_map/exchange/pallas_call | solution.py:495
  206.7 0.0 copy-done.1
  206.8 0.8 multiply_subtract_fusion
  207.6 0.7 copy.17
  (12 shorter events, 0.1 us)
Async XLA Ops:
  173.5 13.7 %copy-start = (f32[384,128]{1,0:T(8,128)S(1)}, f32[384,128]{1,0:T(8,128)}, u32[]{:S(2)}) copy-start(f32[384,128]{1,0:T(8,128)} %linear_ref.1) | copy-start | bytes 589828
  187.1 19.6 %copy-start.1 = (f32[384]{0:T(512)S(1)}, f32[384]{0:T(512)}, u32[]{:S(2)}) copy-start(f32[384]{0:T(512)} %param.9) | copy-start | bytes 4612

commit v8 on v6

--- a/solution.py
+++ b/solution.py
@@ -9,8 +9,8 @@
 
 spectrum_center = 2.0
 spectrum_half = 3.0
-unroll_blocks = 4
-apply_group = 4
+unroll_blocks = 8
+apply_group = 8
 list_group = 4
 sum_rows = 128
 ring_groups = 3

time: 209 us -> 207 us (level)
    pallas_call x2, Pallas kernels: 53.9 us -> 48.1 us  [exchange(): pl.pallas_call(functools.partial(exchange_kernel, spread_on), in_specs=[v...]
where the time goes in v8:
time: 207 us
  Pallas kernels  195 us (94%)
  other arithmetic  8.17 us (4%)
  local copies, waits for them, and re-layouts  3 us (1%)
    pallas_call x1, Pallas kernels, gather_all(): pl.pallas_call(gather_kernel, in_specs=[vmem, vmem, vmem], out_specs=[any...  91.7 us
    pallas_call x2, Pallas kernels, exchange(): pl.pallas_call(functools.partial(exchange_kernel, spread_on), in_specs=[v...  48.1 us
    pallas_call x1, Pallas kernels, project_and_apply(): pl.pallas_call(functools.partial(build_kernel, blocks_dev, spread), grid_...  37.8 us
    pallas_call x1, Pallas kernels, apply_again(): pl.pallas_call(functools.partial(apply_kernel_body, blocks_dev, spread),...  17.2 us

profile of v8, /device:TPU:1, one launch (start us, length us, event | category | flops | bytes accessed | tf_op | source)
XLA Modules:
  0.0 207.4 jit_solution(7950149053698976602)
XLA Ops:
  1.3 0.9 select_reduce_fusion.3
  2.2 0.9 select_reduce_fusion.2
  3.1 0.7 select_reduce_fusion.5.slots_ref
  3.8 1.0 fusion.1
  4.9 0.1 reshape.159
  5.0 0.1 reduce_sum.65
  5.1 0.1 copy.12
  5.1 0.2 select_reduce_fusion.1
  5.3 0.1 select_reduce_fusion.4.base_ref
  5.5 0.1 copy.13
  5.5 0.1 add.139
  5.6 0.1 add_add_fusion
  5.7 0.1 add.149
  5.8 0.4 select_reduce_fusion
  6.2 1.1 multiply_subtract_fusion.1
  7.3 1.9 copy.14
  9.2 1.8 pad_maximum_fusion.i_ref
  11.1 91.7 %gather_all.1 = (bf16[16,896,512]{2,1,0:T(8,128)(2,1)}, bf16[16,512,512]{2,1,0:T(8,128)(2,1)}, bf16[8,1920,128]{2,1,0:T(8,128)(2,1)}) custom-call(bf16[2,512,512]{2,1,0:T(8,128)(2,1)} %bitcast.14, bf16[384,512]{1,0:T(8,128)(2,1)} %bitcast.13, bf16[1920,128]{1,0:T(8,128)(2,1)} %pad_maximum_fusion.i_ref), custom_call_target="tpu_custom_call" | custom-call | tf_op jit(solution)/shard_map/gather_all/pallas_call | solution.py:368
  102.8 37.8 %project_and_apply.1 = (bf16[48,512,128]{2,1,0:T(8,128)(2,1)}, f32[48,128,128]{2,1,0:T(8,128)S(1)}) custom-call(s32[24]{0:T(128)S(1)} %select_reduce_fusion.5.slots_ref, s32[576]{0:T(1024)S(1)} %add_select_fusion.members_ref, s32[48]{0:T(128)S(1)} %select_reduce_fusion.4.base_ref, s32[48]{0:T(128)S(1)} %and_select_fusion.2.groups_ref, ...), custom_call_target="tpu_custom_call" | custom-call | tf_op jit(solution)/shard_map/project_and_apply/pallas_call | solution.py:537
  140.6 32.0 %exchange_spread.1 = (f32[384,128]{1,0:T(8,128)S(1)}, bf16[8,384,128]{2,1,0:T(8,128)(2,1)S(1)}) custom-call(f32[16,384,128]{2,1,0:T(8,128)S(1)} %bitcast.10, f32[384,128]{1,0:T(8,128)S(1)} %get-tuple-element.16.linear_ref), custom_call_target="tpu_custom_call" | custom-call | tf_op jit(solution)/shard_map/exchange_spread/pallas_call | solution.py:490
  172.7 0.0 copy-start
  172.7 17.2 %apply_again.1 = f32[48,128,128]{2,1,0:T(8,128)S(1)} custom-call(s32[576]{0:T(1024)S(1)} %add_select_fusion.members_ref, s32[48]{0:T(128)S(1)} %select_reduce_fusion.4.base_ref, s32[48]{0:T(128)S(1)} %and_select_fusion.2.groups_ref, bf16[48,512,128]{2,1,0:T(8,128)(2,1)} %get-tuple-element.14.projected_ref, ...), custom_call_target="tpu_custom_call" | custom-call | tf_op jit(solution)/shard_map/apply_again/pallas_call | solution.py:569
  189.8 0.0 copy-start.1
  189.9 0.0 copy-done
  189.9 16.1 %exchange.1 = f32[384,128]{1,0:T(8,128)S(1)} custom-call(f32[16,384,128]{2,1,0:T(8,128)S(1)} %bitcast.9, f32[384,128]{1,0:T(8,128)S(1)} %copy-done), custom_call_target="tpu_custom_call" | custom-call | tf_op jit(solution)/shard_map/exchange/pallas_call | solution.py:490
  205.9 0.0 copy-done.1
  205.9 0.8 multiply_subtract_fusion
  206.8 0.7 copy.17
  (12 shorter events, 0.1 us)
Async XLA Ops:
  172.7 17.2 %copy-start = (f32[384,128]{1,0:T(8,128)S(1)}, f32[384,128]{1,0:T(8,128)}, u32[]{:S(2)}) copy-start(f32[384,128]{1,0:T(8,128)} %linear_ref.1) | copy-start | bytes 589828
  189.8 16.1 %copy-start.1 = (f32[384]{0:T(512)S(1)}, f32[384]{0:T(512)}, u32[]{:S(2)}) copy-start(f32[384]{0:T(512)} %param.9) | copy-start | bytes 4612
